TPU v7x, 256 devices: a whole 4x4x8 slice. The times are simulated.
256 devices in a mesh: row: 8 (over z_lo, x), col: 32 (over z_hi, y, core).
Axes of the slice: x: 4, y: 4, z: 8 (z_hi: 4, z_lo: 2; z = z_hi * 2 + z_lo), core: 2. Of those that a mesh axis runs over, the one named last changes fastest.
Arguments:
- tokens: bfloat16 [256, 256, 1024], P('row', 'col'), may hold values from -6 to 6
- shifts: int32 [2], replicated, may hold values from 0 to 15
- qkv_weight: bfloat16 [1024, 3, 1024], P('col', None, 'row'), may hold values from -0.1875 to 0.1875
- out_weight: bfloat16 [1024, 1024], P('row', 'col'), may hold values from -0.1875 to 0.1875
- up_weight: bfloat16 [1024, 4096], P('col', 'row'), may hold values from -0.1875 to 0.1875
- down_weight: bfloat16 [4096, 1024], P('row', 'col'), may hold values from -0.09375 to 0.09375
- qk_gain: float32 [1024], P('row'), may hold values from 0.5 to 1.5
- attn_rate: float32 [1024], replicated, may hold values from 0.1 to 0.6
- mlp_rate: float32 [1024], replicated, may hold values from 0.1 to 0.6
- hidden_gain: float32 [4096], P('row'), may hold values from 0.5 to 2
Outputs:
- sphere_out: bfloat16 [256, 256, 1024], P('row', 'col')
Inputs may be any that keep to these rules, and one draw needn't show every extreme that they name: shifts[0] offsets the windows along rows, shifts[1] along columns.
All inputs are finite; a program needn't handle non-finite values.
Results may differ from a plain program's by a relative error of at most 0.012.
Values may be sent and summed in bfloat16 or wider, within the bound.
No kernel may reach another device: no remote copies, remote signals or barrier semaphores. Data moves between devices by JAX's collectives and lax.ppermute only.
A program may use at most 128 MiB of HBM per device.

v0:
```python
import jax
import jax.numpy as jnp
from jax import lax
from jax.experimental import pallas as pl
from jax.experimental.pallas import tpu as pltpu
from jax.sharding import Mesh, PartitionSpec as P


HD = 64
WIN = 16
ROW = ("zlo", "x")
COL = ("zhi", "y", "core")
F32 = jnp.float32
BF16 = jnp.bfloat16
NT = (((1,), (1,)), ((), ()))


def from_offset(value, axis, offset):
    n = lax.axis_size(axis)
    return lax.ppermute(value, axis, [((i + offset) % n, i) for i in range(n)])


def swapped(value, axis="core"):
    return lax.ppermute(value, axis, [(0, 1), (1, 0)])


def across_edge(value):
    n = lax.axis_size(COL)
    pairs = [((c - 1 if c % 2 == 0 else c + 1) % n, c) for c in range(n)]
    return lax.ppermute(value, COL, pairs)


def direct4(value, axis):
    return [value] + [from_offset(value, axis, d) for d in (1, 2, 3)]


def ring4(value, axis):
    nxt = from_offset(value, axis, 1)
    prv = from_offset(value, axis, -1)
    return [value, nxt, from_offset(nxt, axis, 1), prv]


def call(kernel, outs, *args, scratch=()):
    specs = [pl.BlockSpec(memory_space=pltpu.SMEM)] + [
        pl.BlockSpec(memory_space=pltpu.VMEM) for _ in args[1:]
    ]
    single = not isinstance(outs, (list, tuple))
    out = pl.pallas_call(
        kernel,
        out_shape=outs,
        in_specs=specs,
        out_specs=jax.tree.map(lambda _: pl.BlockSpec(memory_space=pltpu.VMEM), outs),
        scratch_shapes=list(scratch),
        compiler_params=pltpu.CompilerParams(vmem_limit_bytes=48 * 2**20),
    )(*args)
    return out if single else tuple(out)


def sds(shape, dtype):
    return jax.ShapeDtypeStruct(shape, dtype)


def norm(v):
    return v * lax.rsqrt(jnp.mean(v * v, axis=-1, keepdims=True) + 1e-06)


def to_relative(v, y):
    return pltpu.roll(v, lax.rem(256 - 64 * y, 256), 1)


def to_absolute(v, y):
    return pltpu.roll(v, 64 * y, 1)


def pack_kernel(pos, qkv, out_t, up, down_t, keep, send):
    first = pos[0] == 0

    def put(i, lo, hi):
        keep[i] = jnp.where(first, lo, hi)
        send[i] = jnp.where(first, hi, lo)

    q, k, v, o = qkv[0].astype(F32), qkv[1].astype(F32), qkv[2].astype(F32), out_t[...].astype(F32)

    def pair(i, a, b):
        lo = jnp.concatenate([a[:, :64], b[:, :64]], 1).astype(BF16)
        hi = jnp.concatenate([a[:, 64:], b[:, 64:]], 1).astype(BF16)
        put(i, lo, hi)

    pair(0, q, k)
    put(1, down_t[:, :128], down_t[:, 256:384])
    put(2, up[:, :128], up[:, 256:384])
    pair(3, v, o)
    put(4, down_t[:, 128:256], down_t[:, 384:])
    put(5, up[:, 128:256], up[:, 384:])


def rows_kernel(pos, keep, recv, qk_gain, hidden_gain, wide):
    first = pos[0] == 0
    mine = pl.multiple_of(pos[0] * 32, 32)
    other = pl.multiple_of(32 - pos[0] * 32, 32)
    for i in range(6):
        wide[pl.ds(64 * i + mine, 32)] = keep[i]
        wide[pl.ds(64 * i + other, 32)] = recv[i]
    g = qk_gain[...]
    lane = lax.broadcasted_iota(jnp.int32, g.shape, 1)
    turned = pltpu.roll(g, HD, 1)
    g = jnp.where(first == (lane < HD), g, turned)
    h = hidden_gain[...]
    rest = jnp.concatenate([g, jnp.where(first, h[:2], h[2:]), jnp.zeros((5, 128), F32)], 0)
    parts = []
    for _ in range(3):
        parts.append(rest.astype(BF16).astype(F32))
        rest = rest - parts[-1]
    parts.append(jnp.zeros((8, 128), F32))
    wide[384:] = jnp.concatenate(parts, 0).astype(BF16)


def attn_kernel(pos, win, gain, *refs):
    qk, vo, part, (xs, qs, ks, vs, att) = refs[:4], refs[4:8], refs[8], refs[9:]
    zhi, y = pos[2], pos[3]
    s = norm(win[...].astype(F32))
    for z in range(4):
        slab = to_relative(s[:, 256 * z : 256 * z + 256], y)
        xs[lax.rem(z + 4 - zhi, 4)] = slab.astype(BF16)
    x = jnp.concatenate([xs[i] for i in range(4)], 1)
    group = lax.broadcasted_iota(jnp.int32, (256, 256), 0) // HD
    mean = jnp.where(group == lax.broadcasted_iota(jnp.int32, (256, 256), 1) // HD, 1 / HD, 0.0)
    mean = mean.astype(BF16)
    lane = lax.broadcasted_iota(jnp.int32, (512, 128), 1)
    ones = jnp.ones((256, 128), BF16)
    zero = jnp.zeros((512, 128), F32)
    for dx in range(4):

        def stacked(block):
            return jnp.concatenate(
                [
                    jnp.concatenate([block(z, dy, a) for z in range(4) for dy in range(4)], 0)
                    for a in range(2)
                ],
                1,
            )

        wqk = stacked(lambda z, dy, a: qk[dx][dy, z, a])
        wvo = stacked(lambda z, dy, a: vo[dy][dx, z, a])
        pqk = jnp.dot(x, wqk, preferred_element_type=F32)
        pv = jnp.dot(x, wvo, preferred_element_type=F32)
        square = pqk * pqk
        high = square.astype(BF16)
        low = (square - high.astype(F32)).astype(BF16)
        level = jnp.dot(high, mean, preferred_element_type=F32)
        level = level + jnp.dot(low, mean, preferred_element_type=F32)
        pqk = pqk * lax.rsqrt(level + 1e-06)
        for a in range(2):
            both = pqk[:, 128 * a : 128 * a + 128] * gain[a * 4 + dx][None]
            head = a * 4 + dx
            qs[head] = jnp.where(lane < HD, both * (HD**-0.5), zero).astype(BF16)
            ks[head] = pltpu.roll(both, HD, 1).astype(BF16)
            v = pltpu.roll(pv[:, 128 * a : 128 * a + 128], HD, 1)
            vs[head] = jnp.where(lane < HD, zero, v).astype(BF16)

    def heads(i, carry):
        for head in (2 * i, 2 * i + 1):
            for w in range(2):
                t = slice(256 * w, 256 * w + 256)
                score = lax.dot_general(qs[head, t], ks[head, t], NT, preferred_element_type=F32)
                e = jnp.exp(score).astype(BF16)
                rhs = jnp.concatenate([vs[head, t], ones], 1)
                o = jnp.dot(e, rhs, preferred_element_type=F32)
                at = pl.multiple_of(128 * head, 128)
                att[t, pl.ds(at, 128)] = (o[:, :128] / o[:, 128:]).astype(BF16)
        return carry

    lax.fori_loop(0, 4, heads, 0)

    def project(z, carry):
        rhs = jnp.concatenate(
            [
                jnp.concatenate([vo[dy][dx, z, a] for dy in range(4)], 0)
                for a in range(2)
                for dx in range(4)
            ],
            1,
        )
        r = lax.dot_general(att[...], rhs, NT, preferred_element_type=F32)
        at = pl.multiple_of(lax.rem(z + zhi, 4) * 256, 256)
        part[:, pl.ds(at, 256)] = to_absolute(r, y).astype(BF16)
        return carry

    lax.fori_loop(0, 4, project, 0)


def mix_kernel(pos, tokens, attn, rate, mixed, mx):
    zhi, y = pos[2], pos[3]

    def chunk(i, carry):
        t = pl.ds(pl.multiple_of(128 * i, 128), 128)
        s = norm(tokens[t].astype(F32))
        m = norm(s + rate[...] * (norm(attn[t].astype(F32)) - s))
        mixed[t] = m
        for z in range(4):
            slab = to_relative(m[:, 256 * z : 256 * z + 256], y)
            mx[lax.rem(z + 4 - zhi, 4), t] = slab.astype(BF16)
        return carry

    lax.fori_loop(0, 2, chunk, 0)


def up_kernel(pos, own, other, gain, *refs):
    over_x, over_y, act = refs[:4], refs[4:8], refs[8]
    x = jnp.concatenate(
        [jnp.concatenate([half[z] for z in range(4)], 1) for half in (own, other)], 0
    )
    for a in range(2):
        for dx in range(4):
            blocks = [(z, dy) for z in range(4) for dy in range(4)]
            w = jnp.concatenate(
                [
                    jnp.concatenate(
                        [over_x[dx][1, dy, z, a] for z, dy in blocks], 0
                    ),
                    jnp.concatenate(
                        [over_y[dy][1, dx, z, a] for z, dy in blocks], 0
                    ),
                ],
                1,
            )
            unit = a * 4 + dx
            r = jnp.dot(x, w, preferred_element_type=F32) * gain[unit][None]
            r = 0.5 * r * (1.0 + lax.erf(r * (0.5**0.5)))
            act[:, 256 * unit : 256 * unit + 256] = r.astype(BF16)


def down_kernel(pos, act, *refs):
    over_x, over_y, own, other = refs[:4], refs[4:8], refs[8], refs[9]
    zhi, y = pos[2], pos[3]

    x = act[...]
    for z in range(4):
        rhs = []
        for a in range(2):
            for dx in range(4):
                lo = [over_x[dx][0, dy, z, a] for dy in range(4)]
                hi = [over_y[dy][0, dx, z, a] for dy in range(4)]
                rhs += [jnp.concatenate(lo, 0), jnp.concatenate(hi, 0)]
        r = lax.dot_general(x, jnp.concatenate(rhs, 1), NT, preferred_element_type=F32)
        r = to_absolute(r, y)
        at = pl.multiple_of(lax.rem(z + zhi, 4) * 256, 256)
        own[:, pl.ds(at, 256)] = r[:256]
        other[:, pl.ds(at, 256)] = r[256:].astype(BF16)


def last_kernel(pos, own, recv, mixed, rate, out):
    def chunk(i, carry):
        t = pl.ds(pl.multiple_of(128 * i, 128), 128)
        m = mixed[t]
        mlp = own[t] + recv[t].astype(F32)
        out[t] = norm(m + rate[...] * (norm(mlp) - m)).astype(BF16)
        return carry

    lax.fori_loop(0, 2, chunk, 0)


def layer(
    tokens, shifts, qkv_weight, out_weight, up_weight, down_weight, qk_gain, attn_rate, mlp_rate, hidden_gain
):
    core = lax.axis_index("core")
    first = core == 0
    pos = jnp.stack([core] + [lax.axis_index(n) for n in ("zlo", "zhi", "y")])
    pos = pos.astype(jnp.int32)
    rows, cols, width = tokens.shape
    count = rows * cols

    six = sds((6, 32, 128), BF16)
    keep, send = call(
        pack_kernel,
        (six, six),
        pos,
        jnp.transpose(qkv_weight, (1, 0, 2)),
        out_weight.T,
        up_weight,
        down_weight.T,
    )
    wide = call(
        rows_kernel,
        sds((416, 128), BF16),
        pos,
        keep,
        swapped(send),
        qk_gain.reshape(1, 128),
        hidden_gain.reshape(4, 128),
    )

    pair = jnp.stack([wide, swapped(wide, "zlo")])
    gains = pair[:, 384:]
    quad = direct4(pair[:, :384], "zhi")
    one = jnp.stack([b[:, :192] for b in quad])
    two = jnp.concatenate([b[:, 192:].reshape(384, 128) for b in quad] + [gains.reshape(64, 128)])
    one = direct4(one, "y")
    two = direct4(two, "x")
    gains = jnp.stack([b[1536:].reshape(2, 4, 8, 128) for b in two], 1).astype(F32)
    gains = gains[:, :, 0] + gains[:, :, 1] + gains[:, :, 2]
    head_gain = gains[:, :, 0].reshape(8, 128)
    unit_gain = gains[:, :, 1:3].reshape(8, 256)
    two = [b[:1536].reshape(4, 2, 192, 128) for b in two]
    qk = direct4(jnp.stack([b[:, :, :64] for b in one]), "x")
    vo = direct4(jnp.stack([b[:, :, :64] for b in two]), "y")

    shift_row = shifts[0]
    shift_col = jnp.where(shifts[1] > 8, shifts[1] - WIN, shifts[1])
    nxt_rows = from_offset(tokens[:WIN], ROW, 1)
    rolled = lax.dynamic_slice_in_dim(jnp.concatenate([tokens, nxt_rows], 0), shift_row, rows, 0)
    mine = jnp.stack([rolled, across_edge(rolled)])
    theirs = swapped(mine)
    left, right = jnp.where(first, mine, theirs), jnp.where(first, theirs, mine)
    ext = jnp.concatenate([left[1], left[0], right[0], right[1]], axis=1)
    win = lax.dynamic_slice_in_dim(ext, cols + shift_col, WIN, 1).reshape(2 * count, width)

    mlp_x = jnp.stack([b[:, :, i : i + 64] for i in (64, 128) for b in one])
    mlp_y = jnp.stack([b[:, :, i : i + 64] for i in (64, 128) for b in two])
    mlp_x, mlp_y = (m.reshape(2, 4, *m.shape[1:]) for m in (mlp_x, mlp_y))
    win, mlp_x, mlp_y = lax.optimization_barrier((win, mlp_x, mlp_y))
    mlp_x = ring4(mlp_x, "x")
    mlp_y = ring4(mlp_y, "y")

    part = call(
        attn_kernel,
        sds((2 * count, width), BF16),
        pos,
        win,
        head_gain,
        *qk,
        *vo,
        scratch=[pltpu.VMEM((4, 2 * count, 256), BF16)]
        + [pltpu.VMEM((8, 2 * count, 128), BF16)] * 3
        + [pltpu.VMEM((2 * count, 1024), BF16)],
    )
    full = (part.astype(F32) + swapped(part).astype(F32)).astype(BF16)
    full = full.reshape(rows, WIN, width)

    halo = across_edge(jnp.where(first, full[:, :cols], full[:, cols:]))
    ext = jnp.where(
        first, jnp.concatenate([halo, full], axis=1), jnp.concatenate([full, halo], axis=1)
    )
    strip = lax.dynamic_slice_in_dim(ext, cols - shift_col, cols, 1)
    prev_rows = from_offset(strip[rows - WIN :], ROW, -1)
    attn = lax.dynamic_slice_in_dim(
        jnp.concatenate([prev_rows, strip], 0), WIN - shift_row, rows, 0
    ).reshape(count, width)

    mixed, mx = call(
        mix_kernel,
        (sds((count, width), F32), sds((4, count, 256), BF16)),
        pos,
        tokens.reshape(count, width),
        attn,
        attn_rate.reshape(1, width),
    )
    act = call(
        up_kernel, sds((2 * count, 2048), BF16), pos, mx, swapped(mx), unit_gain, *mlp_x, *mlp_y
    )
    own, other = call(
        down_kernel, (sds((count, width), F32), sds((count, width), BF16)), pos, act, *mlp_x, *mlp_y
    )
    result = call(
        last_kernel,
        sds((count, width), BF16),
        pos,
        own,
        swapped(other),
        mixed,
        mlp_rate.reshape(1, width),
    )
    return result.reshape(rows, cols, width)


def solution(mesh):
    fine = Mesh(mesh.devices.reshape(2, 4, 4, 4, 2), ("zlo", "x", "zhi", "y", "core"))
    return jax.shard_map(
        layer,
        mesh=fine,
        in_specs=(
            P(ROW, COL, None),
            P(),
            P(COL, None, ROW),
            P(ROW, COL),
            P(COL, ROW),
            P(ROW, COL),
            P(ROW),
            P(),
            P(),
            P(ROW),
        ),
        out_specs=P(ROW, COL, None),
        check_vma=False,
    )
```

profile of v0, /device:TPU:1, one launch (start us, length us, event | category | flops | bytes accessed | tf_op | source)
XLA Modules:
  0.0 209.3 jit_solution(17726706671442261401)
XLA Ops:
  3.7 3.3 %collective-permute-start.3 = (bf16[6,32,128]{2,1,0:T(8,128)(2,1)S(1)}, bf16[6,32,128]{2,1,0:T(8,128)(2,1)S(1)}, u32[]{:S(2)}, u32[]{:S(2)}) collective-permute-start(bf16[6,32,128]{2,1,0:T(8,128)(2,1)S(1)} %get-tuple-element.15), channel_id=1, source_target_pairs={{0,1},{1,0},{2,3},{3,2},{4,5},{5,4},{6,7},{7,6},{8,9},{9,8},{10,11... | collective-permute-start | bytes 147464 | tf_op jit(solution)/shard_map/ppermute | solution.py:24
  8.0 2.2 %collective-permute-start = (bf16[16,8,1024]{2,1,0:T(8,128)(2,1)S(1)}, bf16[16,8,1024]{2,1,0:T(8,128)(2,1)S(1)}, u32[]{:S(2)}, u32[]{:S(2)}) collective-permute-start(bf16[16,8,1024]{2,1,0:T(8,128)(2,1)S(1)} %slice.171), channel_id=1, source_target_pairs={{32,0},{64,32},{96,64},{128,96},{160,128},{192,160},{224,192},{0,2... | collective-permute-start | bytes 786440 | tf_op jit(solution)/shard_map/ppermute | solution.py:20
  18.7 3.1 %collective-permute-start.7 = (bf16[2,384,128]{2,1,0:T(8,128)(2,1)S(1)}, bf16[2,384,128]{2,1,0:T(8,128)(2,1)S(1)}, u32[]{:S(2)}, u32[]{:S(2)}) collective-permute-start(bf16[2,384,128]{2,1,0:T(8,128)(2,1)S(1)} %fusion.9), channel_id=1, source_target_pairs={{24,0},{0,8},{8,16},{16,24},{25,1},{1,9},{9,17},{17,25},{26,2},{2,... | collective-permute-start | bytes 589832 | tf_op jit(solution)/shard_map/ppermute | solution.py:20
  21.8 5.1 %collective-permute-start.6 = (bf16[2,384,128]{2,1,0:T(8,128)(2,1)S(1)}, bf16[2,384,128]{2,1,0:T(8,128)(2,1)S(1)}, u32[]{:S(2)}, u32[]{:S(2)}) collective-permute-start(bf16[2,384,128]{2,1,0:T(8,128)(2,1)S(1)} %fusion.9), channel_id=1, source_target_pairs={{16,0},{24,8},{0,16},{8,24},{17,1},{25,9},{1,17},{9,25},{18,2},{26... | collective-permute-start | bytes 589832 | tf_op jit(solution)/shard_map/ppermute | solution.py:20
  26.9 2.4 %collective-permute-start.5 = (bf16[2,384,128]{2,1,0:T(8,128)(2,1)S(1)}, bf16[2,384,128]{2,1,0:T(8,128)(2,1)S(1)}, u32[]{:S(2)}, u32[]{:S(2)}) collective-permute-start(bf16[2,384,128]{2,1,0:T(8,128)(2,1)S(1)} %fusion.9), channel_id=1, source_target_pairs={{8,0},{16,8},{24,16},{0,24},{9,1},{17,9},{25,17},{1,25},{10,2},{18... | collective-permute-start | bytes 589832 | tf_op jit(solution)/shard_map/ppermute | solution.py:20
  29.5 3.0 %collective-permute-start.1 = (bf16[32,8,1024]{2,1,0:T(8,128)(2,1)S(1)}, bf16[32,8,1024]{2,1,0:T(8,128)(2,1)S(1)}, u32[]{:S(2)}, u32[]{:S(2)}) collective-permute-start(bf16[32,8,1024]{2,1,0:T(8,128)(2,1)S(1)} %fusion.5), channel_id=1, source_target_pairs={{31,0},{2,1},{1,2},{4,3},{3,4},{6,5},{5,6},{8,7},{7,8},{10,9},{9,1... | collective-permute-start | bytes 1572872 | tf_op jit(solution)/shard_map/ppermute | solution.py:30
  32.5 5.3 %collective-permute-done.6 = bf16[2,384,128]{2,1,0:T(8,128)(2,1)S(1)} collective-permute-done((bf16[2,384,128]{2,1,0:T(8,128)(2,1)S(1)}, bf16[2,384,128]{2,1,0:T(8,128)(2,1)S(1)}, u32[]{:S(2)}, u32[]{:S(2)}) %collective-permute-start.6) | collective-permute-done | bytes 196640 | tf_op jit(solution)/shard_map/ppermute | solution.py:20
  37.8 13.3 %collective-permute-done.5 = bf16[2,384,128]{2,1,0:T(8,128)(2,1)S(1)} collective-permute-done((bf16[2,384,128]{2,1,0:T(8,128)(2,1)S(1)}, bf16[2,384,128]{2,1,0:T(8,128)(2,1)S(1)}, u32[]{:S(2)}, u32[]{:S(2)}) %collective-permute-start.5) | collective-permute-done | bytes 196640 | tf_op jit(solution)/shard_map/ppermute | solution.py:20
  51.4 2.6 %collective-permute-start.8 = (bf16[4,2,192,128]{3,2,1,0:T(8,128)(2,1)S(1)}, bf16[4,2,192,128]{3,2,1,0:T(8,128)(2,1)S(1)}, u32[]{:S(2)}, u32[]{:S(2)}) collective-permute-start(bf16[4,2,192,128]{3,2,1,0:T(8,128)(2,1)S(1)} %pad_maximum_fusion.3), channel_id=1, source_target_pairs={{2,0},{4,2},{6,4},{0,6},{3,1},{5,3},{7,5},{1,7},{10,8},{12,10},{14... | collective-permute-start | bytes 1179656 | tf_op jit(solution)/shard_map/ppermute | solution.py:20
  54.9 16.2 %collective-permute-done.10 = bf16[4,2,192,128]{3,2,1,0:T(8,128)(2,1)S(1)} collective-permute-done((bf16[4,2,192,128]{3,2,1,0:T(8,128)(2,1)S(1)}, bf16[4,2,192,128]{3,2,1,0:T(8,128)(2,1)S(1)}, u32[]{:S(2)}, u32[]{:S(2)}) %collective-permute-start.10) | collective-permute-done | bytes 393248 | tf_op jit(solution)/shard_map/ppermute | solution.py:20
  73.1 3.1 %collective-permute-start.15 = (bf16[4,4,2,64,128]{4,3,2,1,0:T(8,128)(2,1)S(1)}, bf16[4,4,2,64,128]{4,3,2,1,0:T(8,128)(2,1)S(1)}, u32[]{:S(2)}, u32[]{:S(2)}) collective-permute-start(bf16[4,4,2,64,128]{4,3,2,1,0:T(8,128)(2,1)S(1)} %pad_maximum_fusion.1.refs_0_), channel_id=1, source_target_pairs={{64,0},{96,32},{0,64},{32,96},{65,1},{97,33},{1,65},{33,97},{66,2}... | collective-permute-start | bytes 1572872 | tf_op jit(solution)/shard_map/ppermute | solution.py:20
  76.1 6.2 %collective-permute-done.12 = bf16[1600,128]{1,0:T(8,128)(2,1)S(1)} collective-permute-done((bf16[1600,128]{1,0:T(8,128)(2,1)S(1)}, bf16[1600,128]{1,0:T(8,128)(2,1)S(1)}, u32[]{:S(2)}, u32[]{:S(2)}) %collective-permute-start.12) | collective-permute-done | bytes 409632 | tf_op jit(solution)/shard_map/ppermute | solution.py:20
  82.3 6.7 %collective-permute-done.11 = bf16[1600,128]{1,0:T(8,128)(2,1)S(1)} collective-permute-done((bf16[1600,128]{1,0:T(8,128)(2,1)S(1)}, bf16[1600,128]{1,0:T(8,128)(2,1)S(1)}, u32[]{:S(2)}, u32[]{:S(2)}) %collective-permute-start.11) | collective-permute-done | bytes 409632 | tf_op jit(solution)/shard_map/ppermute | solution.py:20
  91.0 2.3 %collective-permute-start.2 = (bf16[2,32,8,1024]{3,2,1,0:T(8,128)(2,1)S(1)}, bf16[2,32,8,1024]{3,2,1,0:T(8,128)(2,1)S(1)}, u32[]{:S(2)}, u32[]{:S(2)}) collective-permute-start(bf16[2,32,8,1024]{3,2,1,0:T(8,128)(2,1)S(1)} %pad_maximum_fusion), channel_id=1, source_target_pairs={{0,1},{1,0},{2,3},{3,2},{4,5},{5,4},{6,7},{7,6},{8,9},{9,8},{10,11... | collective-permute-start | bytes 3145736 | tf_op jit(solution)/shard_map/ppermute | solution.py:24
  96.9 2.1 %collective-permute-start.18 = (bf16[4,4,2,64,128]{4,3,2,1,0:T(8,128)(2,1)S(1)}, bf16[4,4,2,64,128]{4,3,2,1,0:T(8,128)(2,1)S(1)}, u32[]{:S(2)}, u32[]{:S(2)}) collective-permute-start(bf16[4,4,2,64,128]{4,3,2,1,0:T(8,128)(2,1)S(1)} %pad_maximum_fusion.2.refs_4_), channel_id=1, source_target_pairs={{4,0},{6,2},{0,4},{2,6},{5,1},{7,3},{1,5},{3,7},{12,8},{14,10},{8,... | collective-permute-start | bytes 1572872 | tf_op jit(solution)/shard_map/ppermute | solution.py:20
  100.5 2.2 %fusion.2 = bf16[32,16,1024]{2,1,0:T(8,128)(2,1)} fusion(s32[]{:T(128)S(6)} %select_n.51, bf16[32,8,1024]{2,1,0:T(8,128)(2,1)S(1)} %get-tuple-element.39, bf16[32,8,1024]{2,1,0:T(8,128)(2,1)S(1)} %get-tuple-element.40, bf16[32,8,1024]{2,1,0:T(8,128)(2,1)S(1)} %get-tuple-element.26, bf16[32,8,1024]{2,1,0:T(8,128)(2,1)S(1)} %get-tuple-element.25), kind=kLoop, calls=%fused_computation.11 | loop fusion | flops 4194304 | bytes 3145732 | tf_op jit(solution)/shard_map/concatenate | solution.py:315
  104.8 5.6 %collective-permute-done.14.refs_1_ = bf16[4,4,2,64,128]{4,3,2,1,0:T(8,128)(2,1)S(1)} collective-permute-done((bf16[4,4,2,64,128]{4,3,2,1,0:T(8,128)(2,1)S(1)}, bf16[4,4,2,64,128]{4,3,2,1,0:T(8,128)(2,1)S(1)}, u32[]{:S(2)}, u32[]{:S(2)}) %collective-permute-start.14) | collective-permute-done | bytes 524320 | tf_op jit(solution)/shard_map/ppermute | solution.py:20
  112.4 11.0 %collective-permute-done.17.refs_5_ = bf16[4,4,2,64,128]{4,3,2,1,0:T(8,128)(2,1)S(1)} collective-permute-done((bf16[4,4,2,64,128]{4,3,2,1,0:T(8,128)(2,1)S(1)}, bf16[4,4,2,64,128]{4,3,2,1,0:T(8,128)(2,1)S(1)}, u32[]{:S(2)}, u32[]{:S(2)}) %collective-permute-start.17) | collective-permute-done | bytes 524320 | tf_op jit(solution)/shard_map/ppermute | solution.py:20
  123.4 9.5 %shard_map.102 = bf16[512,1024]{1,0:T(8,128)(2,1)S(1)} custom-call(s32[4]{0:T(128)S(1)} %pad_add_fusion.pos, bf16[512,1024]{1,0:T(8,128)(2,1)} %bitcast.165, f32[8,128]{1,0:T(8,128)S(1)} %bitcast.155, bf16[4,4,2,64,128]{4,3,2,1,0:T(8,128)(2,1)S(1)} %pad_maximum_fusion.1.refs_0_, bf16[4,4,2,64,128]{4,3,2,1,0:T(8,128)(2,1)S(1)} %collective-permute-done.14.refs_1_, ...), custom_call_target="tpu_custom_call" | custom-call | tf_op jit(solution)/shard_map/pallas_call | solution.py:48
  133.9 2.5 %collective-permute-start.24 = (bf16[2,4,4,2,64,128]{5,4,3,2,1,0:T(8,128)(2,1)S(1)}, bf16[2,4,4,2,64,128]{5,4,3,2,1,0:T(8,128)(2,1)S(1)}, u32[]{:S(2)}, u32[]{:S(2)}) collective-permute-start(bf16[2,4,4,2,64,128]{5,4,3,2,1,0:T(8,128)(2,1)S(1)} %bitcast.143), channel_id=1, source_target_pairs={{32,0},{64,32},{96,64},{0,96},{33,1},{65,33},{97,65},{1,97},{34,2}... | collective-permute-start | bytes 3145736 | tf_op jit(solution)/shard_map/ppermute | solution.py:20
  136.3 2.1 %collective-permute-start.27 = (bf16[2,4,4,2,64,128]{5,4,3,2,1,0:T(8,128)(2,1)}, bf16[2,4,4,2,64,128]{5,4,3,2,1,0:T(8,128)(2,1)}, u32[]{:S(2)}, u32[]{:S(2)}) collective-permute-start(bf16[2,4,4,2,64,128]{5,4,3,2,1,0:T(8,128)(2,1)} %bitcast.51.refs_4_), channel_id=1, source_target_pairs={{2,0},{4,2},{6,4},{0,6},{3,1},{5,3},{7,5},{1,7},{10,8},{12,10},{14... | collective-permute-start | bytes 3145736 | tf_op jit(solution)/shard_map/ppermute | solution.py:20
  140.2 18.6 %collective-permute-done.24.refs_1_ = bf16[2,4,4,2,64,128]{5,4,3,2,1,0:T(8,128)(2,1)S(1)} collective-permute-done((bf16[2,4,4,2,64,128]{5,4,3,2,1,0:T(8,128)(2,1)S(1)}, bf16[2,4,4,2,64,128]{5,4,3,2,1,0:T(8,128)(2,1)S(1)}, u32[]{:S(2)}, u32[]{:S(2)}) %collective-permute-start.24) | collective-permute-done | bytes 1048608 | tf_op jit(solution)/shard_map/ppermute | solution.py:20
  158.8 3.5 %collective-permute-start.25 = (bf16[2,4,4,2,64,128]{5,4,3,2,1,0:T(8,128)(2,1)S(1)}, bf16[2,4,4,2,64,128]{5,4,3,2,1,0:T(8,128)(2,1)}, u32[]{:S(2)}, u32[]{:S(2)}) collective-permute-start(bf16[2,4,4,2,64,128]{5,4,3,2,1,0:T(8,128)(2,1)S(1)} %collective-permute-done.24.refs_1_), channel_id=1, source_target_pairs={{32,0},{64,32},{96,64},{0,96},{33,1},{65,33},{97,65},{1,97},{34,2}... | collective-permute-start | bytes 3145736 | tf_op jit(solution)/shard_map/ppermute | solution.py:20
  162.3 4.3 %collective-permute-done.27.refs_5_ = bf16[2,4,4,2,64,128]{5,4,3,2,1,0:T(8,128)(2,1)} collective-permute-done((bf16[2,4,4,2,64,128]{5,4,3,2,1,0:T(8,128)(2,1)}, bf16[2,4,4,2,64,128]{5,4,3,2,1,0:T(8,128)(2,1)}, u32[]{:S(2)}, u32[]{:S(2)}) %collective-permute-start.27) | collective-permute-done | bytes 1048608 | tf_op jit(solution)/shard_map/ppermute | solution.py:20
  166.6 3.4 %collective-permute-start.28 = (bf16[2,4,4,2,64,128]{5,4,3,2,1,0:T(8,128)(2,1)}, bf16[2,4,4,2,64,128]{5,4,3,2,1,0:T(8,128)(2,1)}, u32[]{:S(2)}, u32[]{:S(2)}) collective-permute-start(bf16[2,4,4,2,64,128]{5,4,3,2,1,0:T(8,128)(2,1)} %collective-permute-done.27.refs_5_), channel_id=1, source_target_pairs={{2,0},{4,2},{6,4},{0,6},{3,1},{5,3},{7,5},{1,7},{10,8},{12,10},{14... | collective-permute-start | bytes 3145736 | tf_op jit(solution)/shard_map/ppermute | solution.py:20
  170.0 2.5 %fusion.7 = bf16[32,8,1024]{2,1,0:T(8,128)(2,1)S(1)} fusion(s32[]{:T(128)S(6)} %select_n.54, bf16[32,16,1024]{2,1,0:T(8,128)(2,1)} %bitcast.162, bf16[32,8,1024]{2,1,0:T(8,128)(2,1)} %collective-permute-done.21, pred[]{:T(512)S(6)} %eq.3), kind=kLoop, calls=%fused_computation.23 | loop fusion | flops 2359296 | bytes 2097157 | tf_op jit(solution)/shard_map/jit(_where)/select_n | solution.py:341
  175.3 7.4 %collective-permute-done.22 = bf16[16,8,1024]{2,1,0:T(8,128)(2,1)S(1)} collective-permute-done((bf16[16,8,1024]{2,1,0:T(8,128)(2,1)}, bf16[16,8,1024]{2,1,0:T(8,128)(2,1)S(1)}, u32[]{:S(2)}, u32[]{:S(2)}) %collective-permute-start.22) | collective-permute-done | bytes 262176 | tf_op jit(solution)/shard_map/ppermute | solution.py:20
  186.4 2.5 %collective-permute-start.23 = (bf16[4,256,256]{2,1,0:T(8,128)(2,1)S(1)}, bf16[4,256,256]{2,1,0:T(8,128)(2,1)S(1)}, u32[]{:S(2)}, u32[]{:S(2)}) collective-permute-start(bf16[4,256,256]{2,1,0:T(8,128)(2,1)S(1)} %get-tuple-element.17.own), channel_id=1, source_target_pairs={{0,1},{1,0},{2,3},{3,2},{4,5},{5,4},{6,7},{7,6},{8,9},{9,8},{10,11... | collective-permute-start | bytes 1572872 | tf_op jit(solution)/shard_map/ppermute | solution.py:24
  188.9 2.7 %collective-permute-done.28.refs_6_ = bf16[2,4,4,2,64,128]{5,4,3,2,1,0:T(8,128)(2,1)} collective-permute-done((bf16[2,4,4,2,64,128]{5,4,3,2,1,0:T(8,128)(2,1)}, bf16[2,4,4,2,64,128]{5,4,3,2,1,0:T(8,128)(2,1)}, u32[]{:S(2)}, u32[]{:S(2)}) %collective-permute-start.28) | collective-permute-done | bytes 1048608 | tf_op jit(solution)/shard_map/ppermute | solution.py:20
  191.6 6.4 %shard_map.104.act = bf16[512,2048]{1,0:T(8,128)(2,1)} custom-call(s32[4]{0:T(128)S(1)} %pad_add_fusion.pos, bf16[4,256,256]{2,1,0:T(8,128)(2,1)S(1)} %get-tuple-element.17.own, bf16[4,256,256]{2,1,0:T(8,128)(2,1)S(1)} %collective-permute-done.23.other, f32[8,256]{1,0:T(8,128)S(1)} %bitcast.152, bf16[2,4,4,2,64,128]{5,4,3,2,1,0:T(8,128)(2,1)S(1)} %bitcast.145, ...), custom_call_target="tpu_custom_call" | custom-call | tf_op jit(solution)/shard_map/pallas_call | solution.py:48
  198.0 5.6 %shard_map.105 = (f32[256,1024]{1,0:T(8,128)S(1)}, bf16[256,1024]{1,0:T(8,128)(2,1)S(1)}) custom-call(s32[4]{0:T(128)S(1)} %pad_add_fusion.pos, bf16[512,2048]{1,0:T(8,128)(2,1)} %shard_map.104.act, bf16[2,4,4,2,64,128]{5,4,3,2,1,0:T(8,128)(2,1)S(1)} %bitcast.146, bf16[2,4,4,2,64,128]{5,4,3,2,1,0:T(8,128)(2,1)S(1)} %collective-permute-done.24.refs_1_, ...), custom_call_target="tpu_custom_call" | custom-call | tf_op jit(solution)/shard_map/pallas_call | solution.py:48
  203.6 2.2 %collective-permute-start.30 = (bf16[256,1024]{1,0:T(8,128)(2,1)S(1)}, bf16[256,1024]{1,0:T(8,128)(2,1)S(1)}, u32[]{:S(2)}, u32[]{:S(2)}) collective-permute-start(bf16[256,1024]{1,0:T(8,128)(2,1)S(1)} %get-tuple-element.21), channel_id=1, source_target_pairs={{0,1},{1,0},{2,3},{3,2},{4,5},{5,4},{6,7},{7,6},{8,9},{9,8},{10,11... | collective-permute-start | bytes 1572872 | tf_op jit(solution)/shard_map/ppermute | solution.py:24
  (124 shorter events, 35.0 us)
Async XLA Ops:
  3.7 6.5 %collective-permute-start.3 = (bf16[6,32,128]{2,1,0:T(8,128)(2,1)S(1)}, bf16[6,32,128]{2,1,0:T(8,128)(2,1)S(1)}, u32[]{:S(2)}, u32[]{:S(2)}) collective-permute-start(bf16[6,32,128]{2,1,0:T(8,128)(2,1)S(1)} %get-tuple-element.15), channel_id=1, source_target_pairs={{0,1},{1,0},{2,3},{3,2},{4,5},{5,4},{6,7},{7,6},{8,9},{9,8},{10,11... | collective-permute-start | bytes 147464 | tf_op jit(solution)/shard_map/ppermute | solution.py:24
  8.0 21.3 %collective-permute-start = (bf16[16,8,1024]{2,1,0:T(8,128)(2,1)S(1)}, bf16[16,8,1024]{2,1,0:T(8,128)(2,1)S(1)}, u32[]{:S(2)}, u32[]{:S(2)}) collective-permute-start(bf16[16,8,1024]{2,1,0:T(8,128)(2,1)S(1)} %slice.171), channel_id=1, source_target_pairs={{32,0},{64,32},{96,64},{128,96},{160,128},{192,160},{224,192},{0,2... | collective-permute-start | bytes 786440 | tf_op jit(solution)/shard_map/ppermute | solution.py:20
  12.1 6.5 %collective-permute-start.4 = (bf16[416,128]{1,0:T(8,128)(2,1)S(1)}, bf16[416,128]{1,0:T(8,128)(2,1)S(1)}, u32[]{:S(2)}, u32[]{:S(2)}) collective-permute-start(bf16[416,128]{1,0:T(8,128)(2,1)S(1)} %shard_map.101), channel_id=1, source_target_pairs={{0,128},{128,0},{1,129},{129,1},{2,130},{130,2},{3,131},{131,3},{4... | collective-permute-start | bytes 319496 | tf_op jit(solution)/shard_map/ppermute | solution.py:24
  18.7 13.8 %collective-permute-start.7 = (bf16[2,384,128]{2,1,0:T(8,128)(2,1)S(1)}, bf16[2,384,128]{2,1,0:T(8,128)(2,1)S(1)}, u32[]{:S(2)}, u32[]{:S(2)}) collective-permute-start(bf16[2,384,128]{2,1,0:T(8,128)(2,1)S(1)} %fusion.9), channel_id=1, source_target_pairs={{24,0},{0,8},{8,16},{16,24},{25,1},{1,9},{9,17},{17,25},{26,2},{2,... | collective-permute-start | bytes 589832 | tf_op jit(solution)/shard_map/ppermute | solution.py:20
  21.8 16.0 %collective-permute-start.6 = (bf16[2,384,128]{2,1,0:T(8,128)(2,1)S(1)}, bf16[2,384,128]{2,1,0:T(8,128)(2,1)S(1)}, u32[]{:S(2)}, u32[]{:S(2)}) collective-permute-start(bf16[2,384,128]{2,1,0:T(8,128)(2,1)S(1)} %fusion.9), channel_id=1, source_target_pairs={{16,0},{24,8},{0,16},{8,24},{17,1},{25,9},{1,17},{9,25},{18,2},{26... | collective-permute-start | bytes 589832 | tf_op jit(solution)/shard_map/ppermute | solution.py:20
  26.9 24.2 %collective-permute-start.5 = (bf16[2,384,128]{2,1,0:T(8,128)(2,1)S(1)}, bf16[2,384,128]{2,1,0:T(8,128)(2,1)S(1)}, u32[]{:S(2)}, u32[]{:S(2)}) collective-permute-start(bf16[2,384,128]{2,1,0:T(8,128)(2,1)S(1)} %fusion.9), channel_id=1, source_target_pairs={{8,0},{16,8},{24,16},{0,24},{9,1},{17,9},{25,17},{1,25},{10,2},{18... | collective-permute-start | bytes 589832 | tf_op jit(solution)/shard_map/ppermute | solution.py:20
  29.5 61.4 %collective-permute-start.1 = (bf16[32,8,1024]{2,1,0:T(8,128)(2,1)S(1)}, bf16[32,8,1024]{2,1,0:T(8,128)(2,1)S(1)}, u32[]{:S(2)}, u32[]{:S(2)}) collective-permute-start(bf16[32,8,1024]{2,1,0:T(8,128)(2,1)S(1)} %fusion.5), channel_id=1, source_target_pairs={{31,0},{2,1},{1,2},{4,3},{3,4},{6,5},{5,6},{8,7},{7,8},{10,9},{9,1... | collective-permute-start | bytes 1572872 | tf_op jit(solution)/shard_map/ppermute | solution.py:30
  51.2 19.9 %collective-permute-start.10 = (bf16[4,2,192,128]{3,2,1,0:T(8,128)(2,1)S(1)}, bf16[4,2,192,128]{3,2,1,0:T(8,128)(2,1)S(1)}, u32[]{:S(2)}, u32[]{:S(2)}) collective-permute-start(bf16[4,2,192,128]{3,2,1,0:T(8,128)(2,1)S(1)} %pad_maximum_fusion.3), channel_id=1, source_target_pairs={{6,0},{0,2},{2,4},{4,6},{7,1},{1,3},{3,5},{5,7},{14,8},{8,10},{10,... | collective-permute-start | bytes 1179656 | tf_op jit(solution)/shard_map/ppermute | solution.py:20
  51.3 19.8 %collective-permute-start.9 = (bf16[4,2,192,128]{3,2,1,0:T(8,128)(2,1)S(1)}, bf16[4,2,192,128]{3,2,1,0:T(8,128)(2,1)S(1)}, u32[]{:S(2)}, u32[]{:S(2)}) collective-permute-start(bf16[4,2,192,128]{3,2,1,0:T(8,128)(2,1)S(1)} %pad_maximum_fusion.3), channel_id=1, source_target_pairs={{4,0},{6,2},{0,4},{2,6},{5,1},{7,3},{1,5},{3,7},{12,8},{14,10},{8,... | collective-permute-start | bytes 1179656 | tf_op jit(solution)/shard_map/ppermute | solution.py:20
  51.4 21.2 %collective-permute-start.8 = (bf16[4,2,192,128]{3,2,1,0:T(8,128)(2,1)S(1)}, bf16[4,2,192,128]{3,2,1,0:T(8,128)(2,1)S(1)}, u32[]{:S(2)}, u32[]{:S(2)}) collective-permute-start(bf16[4,2,192,128]{3,2,1,0:T(8,128)(2,1)S(1)} %pad_maximum_fusion.3), channel_id=1, source_target_pairs={{2,0},{4,2},{6,4},{0,6},{3,1},{5,3},{7,5},{1,7},{10,8},{12,10},{14... | collective-permute-start | bytes 1179656 | tf_op jit(solution)/shard_map/ppermute | solution.py:20
  54.1 19.0 %collective-permute-start.13 = (bf16[1600,128]{1,0:T(8,128)(2,1)S(1)}, bf16[1600,128]{1,0:T(8,128)(2,1)S(1)}, u32[]{:S(2)}, u32[]{:S(2)}) collective-permute-start(bf16[1600,128]{1,0:T(8,128)(2,1)S(1)} %constant_dynamic-update-slice_fusion), channel_id=1, source_target_pairs={{96,0},{0,32},{32,64},{64,96},{97,1},{1,33},{33,65},{65,97},{98,2}... | collective-permute-start | bytes 1228808 | tf_op jit(solution)/shard_map/ppermute | solution.py:20
  71.1 11.2 %collective-permute-start.12 = (bf16[1600,128]{1,0:T(8,128)(2,1)S(1)}, bf16[1600,128]{1,0:T(8,128)(2,1)S(1)}, u32[]{:S(2)}, u32[]{:S(2)}) collective-permute-start(bf16[1600,128]{1,0:T(8,128)(2,1)S(1)} %constant_dynamic-update-slice_fusion), channel_id=1, source_target_pairs={{64,0},{96,32},{0,64},{32,96},{65,1},{97,33},{1,65},{33,97},{66,2}... | collective-permute-start | bytes 1228808 | tf_op jit(solution)/shard_map/ppermute | solution.py:20
  71.1 17.9 %collective-permute-start.11 = (bf16[1600,128]{1,0:T(8,128)(2,1)S(1)}, bf16[1600,128]{1,0:T(8,128)(2,1)S(1)}, u32[]{:S(2)}, u32[]{:S(2)}) collective-permute-start(bf16[1600,128]{1,0:T(8,128)(2,1)S(1)} %constant_dynamic-update-slice_fusion), channel_id=1, source_target_pairs={{32,0},{64,32},{96,64},{0,96},{33,1},{65,33},{97,65},{1,97},{34,2}... | collective-permute-start | bytes 1228808 | tf_op jit(solution)/shard_map/ppermute | solution.py:20
  72.7 24.2 %collective-permute-start.16 = (bf16[4,4,2,64,128]{4,3,2,1,0:T(8,128)(2,1)S(1)}, bf16[4,4,2,64,128]{4,3,2,1,0:T(8,128)(2,1)S(1)}, u32[]{:S(2)}, u32[]{:S(2)}) collective-permute-start(bf16[4,4,2,64,128]{4,3,2,1,0:T(8,128)(2,1)S(1)} %pad_maximum_fusion.1.refs_0_), channel_id=1, source_target_pairs={{96,0},{0,32},{32,64},{64,96},{97,1},{1,33},{33,65},{65,97},{98,2}... | collective-permute-start | bytes 1572872 | tf_op jit(solution)/shard_map/ppermute | solution.py:20
  73.1 31.7 %collective-permute-start.15 = (bf16[4,4,2,64,128]{4,3,2,1,0:T(8,128)(2,1)S(1)}, bf16[4,4,2,64,128]{4,3,2,1,0:T(8,128)(2,1)S(1)}, u32[]{:S(2)}, u32[]{:S(2)}) collective-permute-start(bf16[4,4,2,64,128]{4,3,2,1,0:T(8,128)(2,1)S(1)} %pad_maximum_fusion.1.refs_0_), channel_id=1, source_target_pairs={{64,0},{96,32},{0,64},{32,96},{65,1},{97,33},{1,65},{33,97},{66,2}... | collective-permute-start | bytes 1572872 | tf_op jit(solution)/shard_map/ppermute | solution.py:20
  82.3 28.0 %collective-permute-start.14 = (bf16[4,4,2,64,128]{4,3,2,1,0:T(8,128)(2,1)S(1)}, bf16[4,4,2,64,128]{4,3,2,1,0:T(8,128)(2,1)S(1)}, u32[]{:S(2)}, u32[]{:S(2)}) collective-permute-start(bf16[4,4,2,64,128]{4,3,2,1,0:T(8,128)(2,1)S(1)} %pad_maximum_fusion.1.refs_0_), channel_id=1, source_target_pairs={{32,0},{64,32},{96,64},{0,96},{33,1},{65,33},{97,65},{1,97},{34,2}... | collective-permute-start | bytes 1572872 | tf_op jit(solution)/shard_map/ppermute | solution.py:20
  89.4 21.0 %collective-permute-start.19 = (bf16[4,4,2,64,128]{4,3,2,1,0:T(8,128)(2,1)S(1)}, bf16[4,4,2,64,128]{4,3,2,1,0:T(8,128)(2,1)S(1)}, u32[]{:S(2)}, u32[]{:S(2)}) collective-permute-start(bf16[4,4,2,64,128]{4,3,2,1,0:T(8,128)(2,1)S(1)} %pad_maximum_fusion.2.refs_4_), channel_id=1, source_target_pairs={{6,0},{0,2},{2,4},{4,6},{7,1},{1,3},{3,5},{5,7},{14,8},{8,10},{10,... | collective-permute-start | bytes 1572872 | tf_op jit(solution)/shard_map/ppermute | solution.py:20
  91.0 8.0 %collective-permute-start.2 = (bf16[2,32,8,1024]{3,2,1,0:T(8,128)(2,1)S(1)}, bf16[2,32,8,1024]{3,2,1,0:T(8,128)(2,1)S(1)}, u32[]{:S(2)}, u32[]{:S(2)}) collective-permute-start(bf16[2,32,8,1024]{3,2,1,0:T(8,128)(2,1)S(1)} %pad_maximum_fusion), channel_id=1, source_target_pairs={{0,1},{1,0},{2,3},{3,2},{4,5},{5,4},{6,7},{7,6},{8,9},{9,8},{10,11... | collective-permute-start | bytes 3145736 | tf_op jit(solution)/shard_map/ppermute | solution.py:24
  96.9 15.5 %collective-permute-start.18 = (bf16[4,4,2,64,128]{4,3,2,1,0:T(8,128)(2,1)S(1)}, bf16[4,4,2,64,128]{4,3,2,1,0:T(8,128)(2,1)S(1)}, u32[]{:S(2)}, u32[]{:S(2)}) collective-permute-start(bf16[4,4,2,64,128]{4,3,2,1,0:T(8,128)(2,1)S(1)} %pad_maximum_fusion.2.refs_4_), channel_id=1, source_target_pairs={{4,0},{6,2},{0,4},{2,6},{5,1},{7,3},{1,5},{3,7},{12,8},{14,10},{8,... | collective-permute-start | bytes 1572872 | tf_op jit(solution)/shard_map/ppermute | solution.py:20
  99.0 24.4 %collective-permute-start.17 = (bf16[4,4,2,64,128]{4,3,2,1,0:T(8,128)(2,1)S(1)}, bf16[4,4,2,64,128]{4,3,2,1,0:T(8,128)(2,1)S(1)}, u32[]{:S(2)}, u32[]{:S(2)}) collective-permute-start(bf16[4,4,2,64,128]{4,3,2,1,0:T(8,128)(2,1)S(1)} %pad_maximum_fusion.2.refs_4_), channel_id=1, source_target_pairs={{2,0},{4,2},{6,4},{0,6},{3,1},{5,3},{7,5},{1,7},{10,8},{12,10},{14... | collective-permute-start | bytes 1572872 | tf_op jit(solution)/shard_map/ppermute | solution.py:20
  132.9 5.6 %collective-permute-start.20 = (bf16[512,1024]{1,0:T(8,128)(2,1)S(1)}, bf16[512,1024]{1,0:T(8,128)(2,1)S(1)}, u32[]{:S(2)}, u32[]{:S(2)}) collective-permute-start(bf16[512,1024]{1,0:T(8,128)(2,1)S(1)} %shard_map.102), channel_id=1, source_target_pairs={{0,1},{1,0},{2,3},{3,2},{4,5},{5,4},{6,7},{7,6},{8,9},{9,8},{10,11... | collective-permute-start | bytes 3145736 | tf_op jit(solution)/shard_map/ppermute | solution.py:24
  133.9 24.9 %collective-permute-start.24 = (bf16[2,4,4,2,64,128]{5,4,3,2,1,0:T(8,128)(2,1)S(1)}, bf16[2,4,4,2,64,128]{5,4,3,2,1,0:T(8,128)(2,1)S(1)}, u32[]{:S(2)}, u32[]{:S(2)}) collective-permute-start(bf16[2,4,4,2,64,128]{5,4,3,2,1,0:T(8,128)(2,1)S(1)} %bitcast.143), channel_id=1, source_target_pairs={{32,0},{64,32},{96,64},{0,96},{33,1},{65,33},{97,65},{1,97},{34,2}... | collective-permute-start | bytes 3145736 | tf_op jit(solution)/shard_map/ppermute | solution.py:20
  136.3 30.2 %collective-permute-start.27 = (bf16[2,4,4,2,64,128]{5,4,3,2,1,0:T(8,128)(2,1)}, bf16[2,4,4,2,64,128]{5,4,3,2,1,0:T(8,128)(2,1)}, u32[]{:S(2)}, u32[]{:S(2)}) collective-permute-start(bf16[2,4,4,2,64,128]{5,4,3,2,1,0:T(8,128)(2,1)} %bitcast.51.refs_4_), channel_id=1, source_target_pairs={{2,0},{4,2},{6,4},{0,6},{3,1},{5,3},{7,5},{1,7},{10,8},{12,10},{14... | collective-permute-start | bytes 3145736 | tf_op jit(solution)/shard_map/ppermute | solution.py:20
  139.9 44.0 %copy-start.6 = (f32[1024]{0:T(1024)S(1)}, f32[1024]{0:T(1024)}, u32[]{:S(2)}) copy-start(f32[1024]{0:T(1024)} %param.17) | copy-start | bytes 12292
  139.9 30.1 %collective-permute-start.21 = (bf16[32,8,1024]{2,1,0:T(8,128)(2,1)}, bf16[32,8,1024]{2,1,0:T(8,128)(2,1)}, u32[]{:S(2)}, u32[]{:S(2)}) collective-permute-start(bf16[32,8,1024]{2,1,0:T(8,128)(2,1)} %slice_select_fusion), channel_id=1, source_target_pairs={{31,0},{2,1},{1,2},{4,3},{3,4},{6,5},{5,6},{8,7},{7,8},{10,9},{9,1... | collective-permute-start | bytes 1572872 | tf_op jit(solution)/shard_map/ppermute | solution.py:30
  139.9 49.0 %collective-permute-start.26 = (bf16[2,4,4,2,64,128]{5,4,3,2,1,0:T(8,128)(2,1)S(1)}, bf16[2,4,4,2,64,128]{5,4,3,2,1,0:T(8,128)(2,1)S(1)}, u32[]{:S(2)}, u32[]{:S(2)}) collective-permute-start(bf16[2,4,4,2,64,128]{5,4,3,2,1,0:T(8,128)(2,1)S(1)} %bitcast.144), channel_id=1, source_target_pairs={{96,0},{0,32},{32,64},{64,96},{97,1},{1,33},{33,65},{65,97},{98,2}... | collective-permute-start | bytes 3145736 | tf_op jit(solution)/shard_map/ppermute | solution.py:20
  139.9 49.0 %collective-permute-start.29 = (bf16[2,4,4,2,64,128]{5,4,3,2,1,0:T(8,128)(2,1)}, bf16[2,4,4,2,64,128]{5,4,3,2,1,0:T(8,128)(2,1)}, u32[]{:S(2)}, u32[]{:S(2)}) collective-permute-start(bf16[2,4,4,2,64,128]{5,4,3,2,1,0:T(8,128)(2,1)} %bitcast.51.refs_4_), channel_id=1, source_target_pairs={{6,0},{0,2},{2,4},{4,6},{7,1},{1,3},{3,5},{5,7},{14,8},{8,10},{10,... | collective-permute-start | bytes 3145736 | tf_op jit(solution)/shard_map/ppermute | solution.py:20
  158.8 30.1 %collective-permute-start.25 = (bf16[2,4,4,2,64,128]{5,4,3,2,1,0:T(8,128)(2,1)S(1)}, bf16[2,4,4,2,64,128]{5,4,3,2,1,0:T(8,128)(2,1)}, u32[]{:S(2)}, u32[]{:S(2)}) collective-permute-start(bf16[2,4,4,2,64,128]{5,4,3,2,1,0:T(8,128)(2,1)S(1)} %collective-permute-done.24.refs_1_), channel_id=1, source_target_pairs={{32,0},{64,32},{96,64},{0,96},{33,1},{65,33},{97,65},{1,97},{34,2}... | collective-permute-start | bytes 3145736 | tf_op jit(solution)/shard_map/ppermute | solution.py:20
  166.6 25.0 %collective-permute-start.28 = (bf16[2,4,4,2,64,128]{5,4,3,2,1,0:T(8,128)(2,1)}, bf16[2,4,4,2,64,128]{5,4,3,2,1,0:T(8,128)(2,1)}, u32[]{:S(2)}, u32[]{:S(2)}) collective-permute-start(bf16[2,4,4,2,64,128]{5,4,3,2,1,0:T(8,128)(2,1)} %collective-permute-done.27.refs_5_), channel_id=1, source_target_pairs={{2,0},{4,2},{6,4},{0,6},{3,1},{5,3},{7,5},{1,7},{10,8},{12,10},{14... | collective-permute-start | bytes 3145736 | tf_op jit(solution)/shard_map/ppermute | solution.py:20
  174.0 8.7 %collective-permute-start.22 = (bf16[16,8,1024]{2,1,0:T(8,128)(2,1)}, bf16[16,8,1024]{2,1,0:T(8,128)(2,1)S(1)}, u32[]{:S(2)}, u32[]{:S(2)}) collective-permute-start(bf16[16,8,1024]{2,1,0:T(8,128)(2,1)} %slice.275), channel_id=1, source_target_pairs={{224,0},{0,32},{32,64},{64,96},{96,128},{128,160},{160,192},{192,2... | collective-permute-start | bytes 786440 | tf_op jit(solution)/shard_map/ppermute | solution.py:20
  186.4 5.2 %collective-permute-start.23 = (bf16[4,256,256]{2,1,0:T(8,128)(2,1)S(1)}, bf16[4,256,256]{2,1,0:T(8,128)(2,1)S(1)}, u32[]{:S(2)}, u32[]{:S(2)}) collective-permute-start(bf16[4,256,256]{2,1,0:T(8,128)(2,1)S(1)} %get-tuple-element.17.own), channel_id=1, source_target_pairs={{0,1},{1,0},{2,3},{3,2},{4,5},{5,4},{6,7},{7,6},{8,9},{9,8},{10,11... | collective-permute-start | bytes 1572872 | tf_op jit(solution)/shard_map/ppermute | solution.py:24
  203.6 3.7 %collective-permute-start.30 = (bf16[256,1024]{1,0:T(8,128)(2,1)S(1)}, bf16[256,1024]{1,0:T(8,128)(2,1)S(1)}, u32[]{:S(2)}, u32[]{:S(2)}) collective-permute-start(bf16[256,1024]{1,0:T(8,128)(2,1)S(1)} %get-tuple-element.21), channel_id=1, source_target_pairs={{0,1},{1,0},{2,3},{3,2},{4,5},{5,4},{6,7},{7,6},{8,9},{9,8},{10,11... | collective-permute-start | bytes 1572872 | tf_op jit(solution)/shard_map/ppermute | solution.py:24
  (11 other events, 64.7 us)
where the time goes:
time: 210 us; the launch traced here: 209 us
  waiting for transfers between devices  106 us (50%)
  starting transfers between devices  48.4 us (23%)
  Pallas kernels  26.2 us (12%)
  local copies, waits for them, and re-layouts  15.1 us (7%)
  other arithmetic  7.97 us (4%)
  between operations  5.56 us (3%)
    ppermute x23, waiting for transfers between devices, from_offset(): return lax.ppermute(value, axis, [((i + offset) % n, i) for i in range(n)])  103 us
    ppermute x23, starting transfers between devices, from_offset(): return lax.ppermute(value, axis, [((i + offset) % n, i) for i in range(n)])  34.3 us
    pallas_call x7, Pallas kernels, call(): pl.pallas_call(kernel, out_shape=outs, in_specs=specs, out_specs=jax.tree...  26.2 us
    ppermute x6, starting transfers between devices, swapped(): return lax.ppermute(value, axis, [(0, 1), (1, 0)])  11.2 us
    unnamed x43, local copies, waits for them, and re-layouts  11 us
  transfers between devices with their start and end apart: 31, of which 17 were waited for; matrix products, arithmetic and copies ran while one was open for 8% of the time, Pallas kernels for 1%

commit v1 on v0

--- a/solution.py
+++ b/solution.py
@@ -294,16 +294,16 @@
     gains = pair[:, 384:]
     quad = direct4(pair[:, :384], "zhi")
     one = jnp.stack([b[:, :192] for b in quad])
-    two = jnp.concatenate([b[:, 192:].reshape(384, 128) for b in quad] + [gains.reshape(64, 128)])
+    values = [b[:, 192:256].reshape(128, 128) for b in quad] + [gains.reshape(64, 128)]
+    values = direct4(jnp.concatenate(values), "x")
     one = direct4(one, "y")
-    two = direct4(two, "x")
-    gains = jnp.stack([b[1536:].reshape(2, 4, 8, 128) for b in two], 1).astype(F32)
+    two = direct4(jnp.stack([b[:, 256:] for b in quad]), "x")
+    gains = jnp.stack([b[512:].reshape(2, 4, 8, 128) for b in values], 1).astype(F32)
     gains = gains[:, :, 0] + gains[:, :, 1] + gains[:, :, 2]
     head_gain = gains[:, :, 0].reshape(8, 128)
     unit_gain = gains[:, :, 1:3].reshape(8, 256)
-    two = [b[:1536].reshape(4, 2, 192, 128) for b in two]
     qk = direct4(jnp.stack([b[:, :, :64] for b in one]), "x")
-    vo = direct4(jnp.stack([b[:, :, :64] for b in two]), "y")
+    vo = direct4(jnp.stack([b[:512].reshape(4, 2, 64, 128) for b in values]), "y")
 
     shift_row = shifts[0]
     shift_col = jnp.where(shifts[1] > 8, shifts[1] - WIN, shifts[1])
@@ -316,7 +316,7 @@
     win = lax.dynamic_slice_in_dim(ext, cols + shift_col, WIN, 1).reshape(2 * count, width)
 
     mlp_x = jnp.stack([b[:, :, i : i + 64] for i in (64, 128) for b in one])
-    mlp_y = jnp.stack([b[:, :, i : i + 64] for i in (64, 128) for b in two])
+    mlp_y = jnp.stack([b[:, :, i : i + 64] for i in (0, 64) for b in two])
     mlp_x, mlp_y = (m.reshape(2, 4, *m.shape[1:]) for m in (mlp_x, mlp_y))
     win, mlp_x, mlp_y = lax.optimization_barrier((win, mlp_x, mlp_y))
     mlp_x = ring4(mlp_x, "x")

time: 210 us -> 214 us (1.019)
  starting transfers between devices: 48.4 us -> 55.3 us
  waiting for transfers between devices: 106 us -> 103 us
    ppermute x23 -> x26, starting transfers between devices: 34.3 us -> 38.8 us  [from_offset(): return lax.ppermute(value, axis, [((i + offset) % n, i) for i in range(n)])]
    ppermute x23 -> x26, waiting for transfers between devices: 103 us -> 100 us  [from_offset(): return lax.ppermute(value, axis, [((i + offset) % n, i) for i in range(n)])]
  transfers between devices with their start and end apart: 31 -> 34, of which waited for: 17 -> 16; matrix products, arithmetic and copies ran while one was open for 8% -> 8% of each run, Pallas kernels for 1% -> 1%
where the time goes in v1:
time: 214 us; the launch traced here: 213 us
  waiting for transfers between devices  103 us (48%)
  starting transfers between devices  55.3 us (26%)
  Pallas kernels  26.2 us (12%)
  local copies, waits for them, and re-layouts  14.9 us (7%)
  other arithmetic  7.99 us (4%)
  between operations  5.82 us (3%)
    ppermute x26, waiting for transfers between devices, from_offset(): return lax.ppermute(value, axis, [((i + offset) % n, i) for i in range(n)])  100 us
    ppermute x26, starting transfers between devices, from_offset(): return lax.ppermute(value, axis, [((i + offset) % n, i) for i in range(n)])  38.8 us
    pallas_call x7, Pallas kernels, call(): pl.pallas_call(kernel, out_shape=outs, in_specs=specs, out_specs=jax.tree...  26.2 us
    ppermute x6, starting transfers between devices, swapped(): return lax.ppermute(value, axis, [(0, 1), (1, 0)])  11.5 us
    unnamed x43, local copies, waits for them, and re-layouts  10.9 us
    ppermute x2, starting transfers between devices, across_edge(): return lax.ppermute(value, COL, pairs)  4.98 us
  transfers between devices with their start and end apart: 34, of which 16 were waited for; matrix products, arithmetic and copies ran while one was open for 8% of the time, Pallas kernels for 1%

profile of v1, /device:TPU:1, one launch (start us, length us, event | category | flops | bytes accessed | tf_op | source)
XLA Modules:
  0.0 213.3 jit_solution(11787556017859521017)
XLA Ops:
  3.7 3.3 %collective-permute-start.3 = (bf16[6,32,128]{2,1,0:T(8,128)(2,1)S(1)}, bf16[6,32,128]{2,1,0:T(8,128)(2,1)S(1)}, u32[]{:S(2)}, u32[]{:S(2)}) collective-permute-start(bf16[6,32,128]{2,1,0:T(8,128)(2,1)S(1)} %get-tuple-element.15), channel_id=1, source_target_pairs={{0,1},{1,0},{2,3},{3,2},{4,5},{5,4},{6,7},{7,6},{8,9},{9,8},{10,11... | collective-permute-start | bytes 147464 | tf_op jit(solution)/shard_map/ppermute | solution.py:24
  8.0 2.2 %collective-permute-start = (bf16[16,8,1024]{2,1,0:T(8,128)(2,1)S(1)}, bf16[16,8,1024]{2,1,0:T(8,128)(2,1)S(1)}, u32[]{:S(2)}, u32[]{:S(2)}) collective-permute-start(bf16[16,8,1024]{2,1,0:T(8,128)(2,1)S(1)} %slice.172), channel_id=1, source_target_pairs={{32,0},{64,32},{96,64},{128,96},{160,128},{192,160},{224,192},{0,2... | collective-permute-start | bytes 786440 | tf_op jit(solution)/shard_map/ppermute | solution.py:20
  18.7 3.1 %collective-permute-start.7 = (bf16[2,384,128]{2,1,0:T(8,128)(2,1)S(1)}, bf16[2,384,128]{2,1,0:T(8,128)(2,1)S(1)}, u32[]{:S(2)}, u32[]{:S(2)}) collective-permute-start(bf16[2,384,128]{2,1,0:T(8,128)(2,1)S(1)} %fusion.9), channel_id=1, source_target_pairs={{24,0},{0,8},{8,16},{16,24},{25,1},{1,9},{9,17},{17,25},{26,2},{2,... | collective-permute-start | bytes 589832 | tf_op jit(solution)/shard_map/ppermute | solution.py:20
  21.8 5.1 %collective-permute-start.6 = (bf16[2,384,128]{2,1,0:T(8,128)(2,1)S(1)}, bf16[2,384,128]{2,1,0:T(8,128)(2,1)S(1)}, u32[]{:S(2)}, u32[]{:S(2)}) collective-permute-start(bf16[2,384,128]{2,1,0:T(8,128)(2,1)S(1)} %fusion.9), channel_id=1, source_target_pairs={{16,0},{24,8},{0,16},{8,24},{17,1},{25,9},{1,17},{9,25},{18,2},{26... | collective-permute-start | bytes 589832 | tf_op jit(solution)/shard_map/ppermute | solution.py:20
  26.9 2.4 %collective-permute-start.5 = (bf16[2,384,128]{2,1,0:T(8,128)(2,1)S(1)}, bf16[2,384,128]{2,1,0:T(8,128)(2,1)S(1)}, u32[]{:S(2)}, u32[]{:S(2)}) collective-permute-start(bf16[2,384,128]{2,1,0:T(8,128)(2,1)S(1)} %fusion.9), channel_id=1, source_target_pairs={{8,0},{16,8},{24,16},{0,24},{9,1},{17,9},{25,17},{1,25},{10,2},{18... | collective-permute-start | bytes 589832 | tf_op jit(solution)/shard_map/ppermute | solution.py:20
  29.5 3.0 %collective-permute-start.1 = (bf16[32,8,1024]{2,1,0:T(8,128)(2,1)S(1)}, bf16[32,8,1024]{2,1,0:T(8,128)(2,1)S(1)}, u32[]{:S(2)}, u32[]{:S(2)}) collective-permute-start(bf16[32,8,1024]{2,1,0:T(8,128)(2,1)S(1)} %fusion.5), channel_id=1, source_target_pairs={{31,0},{2,1},{1,2},{4,3},{3,4},{6,5},{5,6},{8,7},{7,8},{10,9},{9,1... | collective-permute-start | bytes 1572872 | tf_op jit(solution)/shard_map/ppermute | solution.py:30
  32.5 5.3 %collective-permute-done.6 = bf16[2,384,128]{2,1,0:T(8,128)(2,1)S(1)} collective-permute-done((bf16[2,384,128]{2,1,0:T(8,128)(2,1)S(1)}, bf16[2,384,128]{2,1,0:T(8,128)(2,1)S(1)}, u32[]{:S(2)}, u32[]{:S(2)}) %collective-permute-start.6) | collective-permute-done | bytes 196640 | tf_op jit(solution)/shard_map/ppermute | solution.py:20
  37.8 13.3 %collective-permute-done.5 = bf16[2,384,128]{2,1,0:T(8,128)(2,1)S(1)} collective-permute-done((bf16[2,384,128]{2,1,0:T(8,128)(2,1)S(1)}, bf16[2,384,128]{2,1,0:T(8,128)(2,1)S(1)}, u32[]{:S(2)}, u32[]{:S(2)}) %collective-permute-start.5) | collective-permute-done | bytes 196640 | tf_op jit(solution)/shard_map/ppermute | solution.py:20
  51.4 2.6 %collective-permute-start.14 = (bf16[576,128]{1,0:T(8,128)(2,1)S(1)}, bf16[576,128]{1,0:T(8,128)(2,1)S(1)}, u32[]{:S(2)}, u32[]{:S(2)}) collective-permute-start(bf16[576,128]{1,0:T(8,128)(2,1)S(1)} %constant_dynamic-update-slice_fusion), channel_id=1, source_target_pairs={{32,0},{64,32},{96,64},{0,96},{33,1},{65,33},{97,65},{1,97},{34,2}... | collective-permute-start | bytes 442376 | tf_op jit(solution)/shard_map/ppermute | solution.py:20
  55.6 5.4 %collective-permute-done.16 = bf16[576,128]{1,0:T(8,128)(2,1)S(1)} collective-permute-done((bf16[576,128]{1,0:T(8,128)(2,1)S(1)}, bf16[576,128]{1,0:T(8,128)(2,1)S(1)}, u32[]{:S(2)}, u32[]{:S(2)}) %collective-permute-start.16) | collective-permute-done | bytes 147488 | tf_op jit(solution)/shard_map/ppermute | solution.py:20
  61.8 4.7 %collective-permute-done.11 = bf16[4,2,128,128]{3,2,1,0:T(8,128)(2,1)S(1)} collective-permute-done((bf16[4,2,128,128]{3,2,1,0:T(8,128)(2,1)S(1)}, bf16[4,2,128,128]{3,2,1,0:T(8,128)(2,1)S(1)}, u32[]{:S(2)}, u32[]{:S(2)}) %collective-permute-start.11) | collective-permute-done | bytes 262176 | tf_op jit(solution)/shard_map/ppermute | solution.py:20
  67.2 5.4 %collective-permute-done.12 = bf16[4,2,128,128]{3,2,1,0:T(8,128)(2,1)S(1)} collective-permute-done((bf16[4,2,128,128]{3,2,1,0:T(8,128)(2,1)S(1)}, bf16[4,2,128,128]{3,2,1,0:T(8,128)(2,1)S(1)}, u32[]{:S(2)}, u32[]{:S(2)}) %collective-permute-start.12) | collective-permute-done | bytes 262176 | tf_op jit(solution)/shard_map/ppermute | solution.py:20
  78.1 2.8 %collective-permute-start.20 = (bf16[4,4,2,64,128]{4,3,2,1,0:T(8,128)(2,1)S(1)}, bf16[4,4,2,64,128]{4,3,2,1,0:T(8,128)(2,1)S(1)}, u32[]{:S(2)}, u32[]{:S(2)}) collective-permute-start(bf16[4,4,2,64,128]{4,3,2,1,0:T(8,128)(2,1)S(1)} %pad_maximum_fusion.2.refs_4_), channel_id=1, source_target_pairs={{2,0},{4,2},{6,4},{0,6},{3,1},{5,3},{7,5},{1,7},{10,8},{12,10},{14... | collective-permute-start | bytes 1572872 | tf_op jit(solution)/shard_map/ppermute | solution.py:20
  81.6 4.7 %collective-permute-start.19 = (bf16[4,4,2,64,128]{4,3,2,1,0:T(8,128)(2,1)S(1)}, bf16[4,4,2,64,128]{4,3,2,1,0:T(8,128)(2,1)S(1)}, u32[]{:S(2)}, u32[]{:S(2)}) collective-permute-start(bf16[4,4,2,64,128]{4,3,2,1,0:T(8,128)(2,1)S(1)} %pad_maximum_fusion.1.refs_0_), channel_id=1, source_target_pairs={{96,0},{0,32},{32,64},{64,96},{97,1},{1,33},{33,65},{65,97},{98,2}... | collective-permute-start | bytes 1572872 | tf_op jit(solution)/shard_map/ppermute | solution.py:20
  86.5 2.5 %collective-permute-start.2 = (bf16[2,32,8,1024]{3,2,1,0:T(8,128)(2,1)S(1)}, bf16[2,32,8,1024]{3,2,1,0:T(8,128)(2,1)S(1)}, u32[]{:S(2)}, u32[]{:S(2)}) collective-permute-start(bf16[2,32,8,1024]{3,2,1,0:T(8,128)(2,1)S(1)} %pad_maximum_fusion), channel_id=1, source_target_pairs={{0,1},{1,0},{2,3},{3,2},{4,5},{5,4},{6,7},{7,6},{8,9},{9,8},{10,11... | collective-permute-start | bytes 3145736 | tf_op jit(solution)/shard_map/ppermute | solution.py:24
  89.1 14.0 %collective-permute-done.22.refs_7_ = bf16[4,4,2,64,128]{4,3,2,1,0:T(8,128)(2,1)S(1)} collective-permute-done((bf16[4,4,2,64,128]{4,3,2,1,0:T(8,128)(2,1)S(1)}, bf16[4,4,2,64,128]{4,3,2,1,0:T(8,128)(2,1)S(1)}, u32[]{:S(2)}, u32[]{:S(2)}) %collective-permute-start.22) | collective-permute-done | bytes 524320 | tf_op jit(solution)/shard_map/ppermute | solution.py:20
  103.0 2.8 %collective-permute-start.18 = (bf16[4,4,2,64,128]{4,3,2,1,0:T(8,128)(2,1)S(1)}, bf16[4,4,2,64,128]{4,3,2,1,0:T(8,128)(2,1)S(1)}, u32[]{:S(2)}, u32[]{:S(2)}) collective-permute-start(bf16[4,4,2,64,128]{4,3,2,1,0:T(8,128)(2,1)S(1)} %pad_maximum_fusion.1.refs_0_), channel_id=1, source_target_pairs={{64,0},{96,32},{0,64},{32,96},{65,1},{97,33},{1,65},{33,97},{66,2}... | collective-permute-start | bytes 1572872 | tf_op jit(solution)/shard_map/ppermute | solution.py:20
  105.8 2.4 %collective-permute-start.17 = (bf16[4,4,2,64,128]{4,3,2,1,0:T(8,128)(2,1)S(1)}, bf16[4,4,2,64,128]{4,3,2,1,0:T(8,128)(2,1)S(1)}, u32[]{:S(2)}, u32[]{:S(2)}) collective-permute-start(bf16[4,4,2,64,128]{4,3,2,1,0:T(8,128)(2,1)S(1)} %pad_maximum_fusion.1.refs_0_), channel_id=1, source_target_pairs={{32,0},{64,32},{96,64},{0,96},{33,1},{65,33},{97,65},{1,97},{34,2}... | collective-permute-start | bytes 1572872 | tf_op jit(solution)/shard_map/ppermute | solution.py:20
  110.7 5.1 %collective-permute-done.18.refs_2_ = bf16[4,4,2,64,128]{4,3,2,1,0:T(8,128)(2,1)S(1)} collective-permute-done((bf16[4,4,2,64,128]{4,3,2,1,0:T(8,128)(2,1)S(1)}, bf16[4,4,2,64,128]{4,3,2,1,0:T(8,128)(2,1)S(1)}, u32[]{:S(2)}, u32[]{:S(2)}) %collective-permute-start.18) | collective-permute-done | bytes 524320 | tf_op jit(solution)/shard_map/ppermute | solution.py:20
  115.8 12.9 %collective-permute-done.17.refs_1_ = bf16[4,4,2,64,128]{4,3,2,1,0:T(8,128)(2,1)S(1)} collective-permute-done((bf16[4,4,2,64,128]{4,3,2,1,0:T(8,128)(2,1)S(1)}, bf16[4,4,2,64,128]{4,3,2,1,0:T(8,128)(2,1)S(1)}, u32[]{:S(2)}, u32[]{:S(2)}) %collective-permute-start.17) | collective-permute-done | bytes 524320 | tf_op jit(solution)/shard_map/ppermute | solution.py:20
  128.7 9.5 %shard_map.102 = bf16[512,1024]{1,0:T(8,128)(2,1)S(1)} custom-call(s32[4]{0:T(128)S(1)} %pad_add_fusion.pos, bf16[512,1024]{1,0:T(8,128)(2,1)} %bitcast.167, f32[8,128]{1,0:T(8,128)S(1)} %bitcast.157, bf16[4,4,2,64,128]{4,3,2,1,0:T(8,128)(2,1)S(1)} %pad_maximum_fusion.1.refs_0_, bf16[4,4,2,64,128]{4,3,2,1,0:T(8,128)(2,1)S(1)} %collective-permute-done.17.refs_1_, ...), custom_call_target="tpu_custom_call" | custom-call | tf_op jit(solution)/shard_map/pallas_call | solution.py:48
  139.9 2.4 %collective-permute-start.27 = (bf16[2,4,4,2,64,128]{5,4,3,2,1,0:T(8,128)(2,1)S(1)}, bf16[2,4,4,2,64,128]{5,4,3,2,1,0:T(8,128)(2,1)S(1)}, u32[]{:S(2)}, u32[]{:S(2)}) collective-permute-start(bf16[2,4,4,2,64,128]{5,4,3,2,1,0:T(8,128)(2,1)S(1)} %bitcast.149), channel_id=1, source_target_pairs={{32,0},{64,32},{96,64},{0,96},{33,1},{65,33},{97,65},{1,97},{34,2}... | collective-permute-start | bytes 3145736 | tf_op jit(solution)/shard_map/ppermute | solution.py:20
  145.6 19.0 %collective-permute-done.27.refs_1_ = bf16[2,4,4,2,64,128]{5,4,3,2,1,0:T(8,128)(2,1)S(1)} collective-permute-done((bf16[2,4,4,2,64,128]{5,4,3,2,1,0:T(8,128)(2,1)S(1)}, bf16[2,4,4,2,64,128]{5,4,3,2,1,0:T(8,128)(2,1)S(1)}, u32[]{:S(2)}, u32[]{:S(2)}) %collective-permute-start.27) | collective-permute-done | bytes 1048608 | tf_op jit(solution)/shard_map/ppermute | solution.py:20
  164.6 3.5 %collective-permute-start.28 = (bf16[2,4,4,2,64,128]{5,4,3,2,1,0:T(8,128)(2,1)S(1)}, bf16[2,4,4,2,64,128]{5,4,3,2,1,0:T(8,128)(2,1)}, u32[]{:S(2)}, u32[]{:S(2)}) collective-permute-start(bf16[2,4,4,2,64,128]{5,4,3,2,1,0:T(8,128)(2,1)S(1)} %collective-permute-done.27.refs_1_), channel_id=1, source_target_pairs={{32,0},{64,32},{96,64},{0,96},{33,1},{65,33},{97,65},{1,97},{34,2}... | collective-permute-start | bytes 3145736 | tf_op jit(solution)/shard_map/ppermute | solution.py:20
  168.1 2.4 %collective-permute-done.30.refs_5_ = bf16[2,4,4,2,64,128]{5,4,3,2,1,0:T(8,128)(2,1)} collective-permute-done((bf16[2,4,4,2,64,128]{5,4,3,2,1,0:T(8,128)(2,1)}, bf16[2,4,4,2,64,128]{5,4,3,2,1,0:T(8,128)(2,1)}, u32[]{:S(2)}, u32[]{:S(2)}) %collective-permute-start.30) | collective-permute-done | bytes 1048608 | tf_op jit(solution)/shard_map/ppermute | solution.py:20
  170.6 3.4 %collective-permute-start.31 = (bf16[2,4,4,2,64,128]{5,4,3,2,1,0:T(8,128)(2,1)}, bf16[2,4,4,2,64,128]{5,4,3,2,1,0:T(8,128)(2,1)}, u32[]{:S(2)}, u32[]{:S(2)}) collective-permute-start(bf16[2,4,4,2,64,128]{5,4,3,2,1,0:T(8,128)(2,1)} %collective-permute-done.30.refs_5_), channel_id=1, source_target_pairs={{2,0},{4,2},{6,4},{0,6},{3,1},{5,3},{7,5},{1,7},{10,8},{12,10},{14... | collective-permute-start | bytes 3145736 | tf_op jit(solution)/shard_map/ppermute | solution.py:20
  174.0 2.5 %fusion.7 = bf16[32,8,1024]{2,1,0:T(8,128)(2,1)S(1)} fusion(s32[]{:T(128)S(6)} %select_n.54, bf16[32,16,1024]{2,1,0:T(8,128)(2,1)} %bitcast.164, bf16[32,8,1024]{2,1,0:T(8,128)(2,1)} %collective-permute-done.24, pred[]{:T(512)S(6)} %eq.3), kind=kLoop, calls=%fused_computation.23 | loop fusion | flops 2359296 | bytes 2097157 | tf_op jit(solution)/shard_map/jit(_where)/select_n | solution.py:341
  179.4 7.6 %collective-permute-done.25 = bf16[16,8,1024]{2,1,0:T(8,128)(2,1)S(1)} collective-permute-done((bf16[16,8,1024]{2,1,0:T(8,128)(2,1)}, bf16[16,8,1024]{2,1,0:T(8,128)(2,1)S(1)}, u32[]{:S(2)}, u32[]{:S(2)}) %collective-permute-start.25) | collective-permute-done | bytes 262176 | tf_op jit(solution)/shard_map/ppermute | solution.py:20
  190.7 2.2 %collective-permute-start.26 = (bf16[4,256,256]{2,1,0:T(8,128)(2,1)S(1)}, bf16[4,256,256]{2,1,0:T(8,128)(2,1)S(1)}, u32[]{:S(2)}, u32[]{:S(2)}) collective-permute-start(bf16[4,256,256]{2,1,0:T(8,128)(2,1)S(1)} %get-tuple-element.17.own), channel_id=1, source_target_pairs={{0,1},{1,0},{2,3},{3,2},{4,5},{5,4},{6,7},{7,6},{8,9},{9,8},{10,11... | collective-permute-start | bytes 1572872 | tf_op jit(solution)/shard_map/ppermute | solution.py:24
  192.9 3.0 %collective-permute-done.31.refs_6_ = bf16[2,4,4,2,64,128]{5,4,3,2,1,0:T(8,128)(2,1)} collective-permute-done((bf16[2,4,4,2,64,128]{5,4,3,2,1,0:T(8,128)(2,1)}, bf16[2,4,4,2,64,128]{5,4,3,2,1,0:T(8,128)(2,1)}, u32[]{:S(2)}, u32[]{:S(2)}) %collective-permute-start.31) | collective-permute-done | bytes 1048608 | tf_op jit(solution)/shard_map/ppermute | solution.py:20
  195.9 6.4 %shard_map.104.act = bf16[512,2048]{1,0:T(8,128)(2,1)} custom-call(s32[4]{0:T(128)S(1)} %pad_add_fusion.pos, bf16[4,256,256]{2,1,0:T(8,128)(2,1)S(1)} %get-tuple-element.17.own, bf16[4,256,256]{2,1,0:T(8,128)(2,1)S(1)} %collective-permute-done.26.other, f32[8,256]{1,0:T(8,128)S(1)} %bitcast.154, bf16[2,4,4,2,64,128]{5,4,3,2,1,0:T(8,128)(2,1)S(1)} %bitcast.151, ...), custom_call_target="tpu_custom_call" | custom-call | tf_op jit(solution)/shard_map/pallas_call | solution.py:48
  202.3 5.6 %shard_map.105 = (f32[256,1024]{1,0:T(8,128)S(1)}, bf16[256,1024]{1,0:T(8,128)(2,1)S(1)}) custom-call(s32[4]{0:T(128)S(1)} %pad_add_fusion.pos, bf16[512,2048]{1,0:T(8,128)(2,1)} %shard_map.104.act, bf16[2,4,4,2,64,128]{5,4,3,2,1,0:T(8,128)(2,1)S(1)} %bitcast.152, bf16[2,4,4,2,64,128]{5,4,3,2,1,0:T(8,128)(2,1)S(1)} %collective-permute-done.27.refs_1_, ...), custom_call_target="tpu_custom_call" | custom-call | tf_op jit(solution)/shard_map/pallas_call | solution.py:48
  (137 shorter events, 37.1 us)
Async XLA Ops:
  3.7 6.5 %collective-permute-start.3 = (bf16[6,32,128]{2,1,0:T(8,128)(2,1)S(1)}, bf16[6,32,128]{2,1,0:T(8,128)(2,1)S(1)}, u32[]{:S(2)}, u32[]{:S(2)}) collective-permute-start(bf16[6,32,128]{2,1,0:T(8,128)(2,1)S(1)} %get-tuple-element.15), channel_id=1, source_target_pairs={{0,1},{1,0},{2,3},{3,2},{4,5},{5,4},{6,7},{7,6},{8,9},{9,8},{10,11... | collective-permute-start | bytes 147464 | tf_op jit(solution)/shard_map/ppermute | solution.py:24
  8.0 21.3 %collective-permute-start = (bf16[16,8,1024]{2,1,0:T(8,128)(2,1)S(1)}, bf16[16,8,1024]{2,1,0:T(8,128)(2,1)S(1)}, u32[]{:S(2)}, u32[]{:S(2)}) collective-permute-start(bf16[16,8,1024]{2,1,0:T(8,128)(2,1)S(1)} %slice.172), channel_id=1, source_target_pairs={{32,0},{64,32},{96,64},{128,96},{160,128},{192,160},{224,192},{0,2... | collective-permute-start | bytes 786440 | tf_op jit(solution)/shard_map/ppermute | solution.py:20
  12.1 6.5 %collective-permute-start.4 = (bf16[416,128]{1,0:T(8,128)(2,1)S(1)}, bf16[416,128]{1,0:T(8,128)(2,1)S(1)}, u32[]{:S(2)}, u32[]{:S(2)}) collective-permute-start(bf16[416,128]{1,0:T(8,128)(2,1)S(1)} %shard_map.101), channel_id=1, source_target_pairs={{0,128},{128,0},{1,129},{129,1},{2,130},{130,2},{3,131},{131,3},{4... | collective-permute-start | bytes 319496 | tf_op jit(solution)/shard_map/ppermute | solution.py:24
  18.7 32.4 %collective-permute-start.7 = (bf16[2,384,128]{2,1,0:T(8,128)(2,1)S(1)}, bf16[2,384,128]{2,1,0:T(8,128)(2,1)S(1)}, u32[]{:S(2)}, u32[]{:S(2)}) collective-permute-start(bf16[2,384,128]{2,1,0:T(8,128)(2,1)S(1)} %fusion.9), channel_id=1, source_target_pairs={{24,0},{0,8},{8,16},{16,24},{25,1},{1,9},{9,17},{17,25},{26,2},{2,... | collective-permute-start | bytes 589832 | tf_op jit(solution)/shard_map/ppermute | solution.py:20
  21.8 16.0 %collective-permute-start.6 = (bf16[2,384,128]{2,1,0:T(8,128)(2,1)S(1)}, bf16[2,384,128]{2,1,0:T(8,128)(2,1)S(1)}, u32[]{:S(2)}, u32[]{:S(2)}) collective-permute-start(bf16[2,384,128]{2,1,0:T(8,128)(2,1)S(1)} %fusion.9), channel_id=1, source_target_pairs={{16,0},{24,8},{0,16},{8,24},{17,1},{25,9},{1,17},{9,25},{18,2},{26... | collective-permute-start | bytes 589832 | tf_op jit(solution)/shard_map/ppermute | solution.py:20
  26.9 24.2 %collective-permute-start.5 = (bf16[2,384,128]{2,1,0:T(8,128)(2,1)S(1)}, bf16[2,384,128]{2,1,0:T(8,128)(2,1)S(1)}, u32[]{:S(2)}, u32[]{:S(2)}) collective-permute-start(bf16[2,384,128]{2,1,0:T(8,128)(2,1)S(1)} %fusion.9), channel_id=1, source_target_pairs={{8,0},{16,8},{24,16},{0,24},{9,1},{17,9},{25,17},{1,25},{10,2},{18... | collective-permute-start | bytes 589832 | tf_op jit(solution)/shard_map/ppermute | solution.py:20
  29.5 56.8 %collective-permute-start.1 = (bf16[32,8,1024]{2,1,0:T(8,128)(2,1)S(1)}, bf16[32,8,1024]{2,1,0:T(8,128)(2,1)S(1)}, u32[]{:S(2)}, u32[]{:S(2)}) collective-permute-start(bf16[32,8,1024]{2,1,0:T(8,128)(2,1)S(1)} %fusion.5), channel_id=1, source_target_pairs={{31,0},{2,1},{1,2},{4,3},{3,4},{6,5},{5,6},{8,7},{7,8},{10,9},{9,1... | collective-permute-start | bytes 1572872 | tf_op jit(solution)/shard_map/ppermute | solution.py:30
  51.2 9.8 %collective-permute-start.16 = (bf16[576,128]{1,0:T(8,128)(2,1)S(1)}, bf16[576,128]{1,0:T(8,128)(2,1)S(1)}, u32[]{:S(2)}, u32[]{:S(2)}) collective-permute-start(bf16[576,128]{1,0:T(8,128)(2,1)S(1)} %constant_dynamic-update-slice_fusion), channel_id=1, source_target_pairs={{96,0},{0,32},{32,64},{64,96},{97,1},{1,33},{33,65},{65,97},{98,2}... | collective-permute-start | bytes 442376 | tf_op jit(solution)/shard_map/ppermute | solution.py:20
  51.3 9.8 %collective-permute-start.15 = (bf16[576,128]{1,0:T(8,128)(2,1)S(1)}, bf16[576,128]{1,0:T(8,128)(2,1)S(1)}, u32[]{:S(2)}, u32[]{:S(2)}) collective-permute-start(bf16[576,128]{1,0:T(8,128)(2,1)S(1)} %constant_dynamic-update-slice_fusion), channel_id=1, source_target_pairs={{64,0},{96,32},{0,64},{32,96},{65,1},{97,33},{1,65},{33,97},{66,2}... | collective-permute-start | bytes 442376 | tf_op jit(solution)/shard_map/ppermute | solution.py:20
  51.4 10.2 %collective-permute-start.14 = (bf16[576,128]{1,0:T(8,128)(2,1)S(1)}, bf16[576,128]{1,0:T(8,128)(2,1)S(1)}, u32[]{:S(2)}, u32[]{:S(2)}) collective-permute-start(bf16[576,128]{1,0:T(8,128)(2,1)S(1)} %constant_dynamic-update-slice_fusion), channel_id=1, source_target_pairs={{32,0},{64,32},{96,64},{0,96},{33,1},{65,33},{97,65},{1,97},{34,2}... | collective-permute-start | bytes 442376 | tf_op jit(solution)/shard_map/ppermute | solution.py:20
  54.0 12.5 %collective-permute-start.11 = (bf16[4,2,128,128]{3,2,1,0:T(8,128)(2,1)S(1)}, bf16[4,2,128,128]{3,2,1,0:T(8,128)(2,1)S(1)}, u32[]{:S(2)}, u32[]{:S(2)}) collective-permute-start(bf16[4,2,128,128]{3,2,1,0:T(8,128)(2,1)S(1)} %pad_maximum_fusion.4), channel_id=1, source_target_pairs={{32,0},{64,32},{96,64},{0,96},{33,1},{65,33},{97,65},{1,97},{34,2}... | collective-permute-start | bytes 786440 | tf_op jit(solution)/shard_map/ppermute | solution.py:20
  61.0 13.8 %collective-permute-start.13 = (bf16[4,2,128,128]{3,2,1,0:T(8,128)(2,1)S(1)}, bf16[4,2,128,128]{3,2,1,0:T(8,128)(2,1)S(1)}, u32[]{:S(2)}, u32[]{:S(2)}) collective-permute-start(bf16[4,2,128,128]{3,2,1,0:T(8,128)(2,1)S(1)} %pad_maximum_fusion.4), channel_id=1, source_target_pairs={{96,0},{0,32},{32,64},{64,96},{97,1},{1,33},{33,65},{65,97},{98,2}... | collective-permute-start | bytes 786440 | tf_op jit(solution)/shard_map/ppermute | solution.py:20
  61.0 11.6 %collective-permute-start.12 = (bf16[4,2,128,128]{3,2,1,0:T(8,128)(2,1)S(1)}, bf16[4,2,128,128]{3,2,1,0:T(8,128)(2,1)S(1)}, u32[]{:S(2)}, u32[]{:S(2)}) collective-permute-start(bf16[4,2,128,128]{3,2,1,0:T(8,128)(2,1)S(1)} %pad_maximum_fusion.4), channel_id=1, source_target_pairs={{64,0},{96,32},{0,64},{32,96},{65,1},{97,33},{1,65},{33,97},{66,2}... | collective-permute-start | bytes 786440 | tf_op jit(solution)/shard_map/ppermute | solution.py:20
  61.6 16.5 %collective-permute-start.10 = (bf16[4,2,192,128]{3,2,1,0:T(8,128)(2,1)S(1)}, bf16[4,2,192,128]{3,2,1,0:T(8,128)(2,1)S(1)}, u32[]{:S(2)}, u32[]{:S(2)}) collective-permute-start(bf16[4,2,192,128]{3,2,1,0:T(8,128)(2,1)S(1)} %pad_maximum_fusion.3), channel_id=1, source_target_pairs={{6,0},{0,2},{2,4},{4,6},{7,1},{1,3},{3,5},{5,7},{14,8},{8,10},{10,... | collective-permute-start | bytes 1179656 | tf_op jit(solution)/shard_map/ppermute | solution.py:20
  66.5 11.6 %collective-permute-start.9 = (bf16[4,2,192,128]{3,2,1,0:T(8,128)(2,1)S(1)}, bf16[4,2,192,128]{3,2,1,0:T(8,128)(2,1)S(1)}, u32[]{:S(2)}, u32[]{:S(2)}) collective-permute-start(bf16[4,2,192,128]{3,2,1,0:T(8,128)(2,1)S(1)} %pad_maximum_fusion.3), channel_id=1, source_target_pairs={{4,0},{6,2},{0,4},{2,6},{5,1},{7,3},{1,5},{3,7},{12,8},{14,10},{8,... | collective-permute-start | bytes 1179656 | tf_op jit(solution)/shard_map/ppermute | solution.py:20
  72.6 8.9 %collective-permute-start.8 = (bf16[4,2,192,128]{3,2,1,0:T(8,128)(2,1)S(1)}, bf16[4,2,192,128]{3,2,1,0:T(8,128)(2,1)S(1)}, u32[]{:S(2)}, u32[]{:S(2)}) collective-permute-start(bf16[4,2,192,128]{3,2,1,0:T(8,128)(2,1)S(1)} %pad_maximum_fusion.3), channel_id=1, source_target_pairs={{2,0},{4,2},{6,4},{0,6},{3,1},{5,3},{7,5},{1,7},{10,8},{12,10},{14... | collective-permute-start | bytes 1179656 | tf_op jit(solution)/shard_map/ppermute | solution.py:20
  74.8 28.2 %collective-permute-start.22 = (bf16[4,4,2,64,128]{4,3,2,1,0:T(8,128)(2,1)S(1)}, bf16[4,4,2,64,128]{4,3,2,1,0:T(8,128)(2,1)S(1)}, u32[]{:S(2)}, u32[]{:S(2)}) collective-permute-start(bf16[4,4,2,64,128]{4,3,2,1,0:T(8,128)(2,1)S(1)} %pad_maximum_fusion.2.refs_4_), channel_id=1, source_target_pairs={{6,0},{0,2},{2,4},{4,6},{7,1},{1,3},{3,5},{5,7},{14,8},{8,10},{10,... | collective-permute-start | bytes 1572872 | tf_op jit(solution)/shard_map/ppermute | solution.py:20
  78.1 32.6 %collective-permute-start.21 = (bf16[4,4,2,64,128]{4,3,2,1,0:T(8,128)(2,1)S(1)}, bf16[4,4,2,64,128]{4,3,2,1,0:T(8,128)(2,1)S(1)}, u32[]{:S(2)}, u32[]{:S(2)}) collective-permute-start(bf16[4,4,2,64,128]{4,3,2,1,0:T(8,128)(2,1)S(1)} %pad_maximum_fusion.2.refs_4_), channel_id=1, source_target_pairs={{4,0},{6,2},{0,4},{2,6},{5,1},{7,3},{1,5},{3,7},{12,8},{14,10},{8,... | collective-permute-start | bytes 1572872 | tf_op jit(solution)/shard_map/ppermute | solution.py:20
  78.1 32.6 %collective-permute-start.20 = (bf16[4,4,2,64,128]{4,3,2,1,0:T(8,128)(2,1)S(1)}, bf16[4,4,2,64,128]{4,3,2,1,0:T(8,128)(2,1)S(1)}, u32[]{:S(2)}, u32[]{:S(2)}) collective-permute-start(bf16[4,4,2,64,128]{4,3,2,1,0:T(8,128)(2,1)S(1)} %pad_maximum_fusion.2.refs_4_), channel_id=1, source_target_pairs={{2,0},{4,2},{6,4},{0,6},{3,1},{5,3},{7,5},{1,7},{10,8},{12,10},{14... | collective-permute-start | bytes 1572872 | tf_op jit(solution)/shard_map/ppermute | solution.py:20
  81.6 29.1 %collective-permute-start.19 = (bf16[4,4,2,64,128]{4,3,2,1,0:T(8,128)(2,1)S(1)}, bf16[4,4,2,64,128]{4,3,2,1,0:T(8,128)(2,1)S(1)}, u32[]{:S(2)}, u32[]{:S(2)}) collective-permute-start(bf16[4,4,2,64,128]{4,3,2,1,0:T(8,128)(2,1)S(1)} %pad_maximum_fusion.1.refs_0_), channel_id=1, source_target_pairs={{96,0},{0,32},{32,64},{64,96},{97,1},{1,33},{33,65},{65,97},{98,2}... | collective-permute-start | bytes 1572872 | tf_op jit(solution)/shard_map/ppermute | solution.py:20
  86.5 19.3 %collective-permute-start.2 = (bf16[2,32,8,1024]{3,2,1,0:T(8,128)(2,1)S(1)}, bf16[2,32,8,1024]{3,2,1,0:T(8,128)(2,1)S(1)}, u32[]{:S(2)}, u32[]{:S(2)}) collective-permute-start(bf16[2,32,8,1024]{3,2,1,0:T(8,128)(2,1)S(1)} %pad_maximum_fusion), channel_id=1, source_target_pairs={{0,1},{1,0},{2,3},{3,2},{4,5},{5,4},{6,7},{7,6},{8,9},{9,8},{10,11... | collective-permute-start | bytes 3145736 | tf_op jit(solution)/shard_map/ppermute | solution.py:24
  103.0 12.7 %collective-permute-start.18 = (bf16[4,4,2,64,128]{4,3,2,1,0:T(8,128)(2,1)S(1)}, bf16[4,4,2,64,128]{4,3,2,1,0:T(8,128)(2,1)S(1)}, u32[]{:S(2)}, u32[]{:S(2)}) collective-permute-start(bf16[4,4,2,64,128]{4,3,2,1,0:T(8,128)(2,1)S(1)} %pad_maximum_fusion.1.refs_0_), channel_id=1, source_target_pairs={{64,0},{96,32},{0,64},{32,96},{65,1},{97,33},{1,65},{33,97},{66,2}... | collective-permute-start | bytes 1572872 | tf_op jit(solution)/shard_map/ppermute | solution.py:20
  105.8 22.9 %collective-permute-start.17 = (bf16[4,4,2,64,128]{4,3,2,1,0:T(8,128)(2,1)S(1)}, bf16[4,4,2,64,128]{4,3,2,1,0:T(8,128)(2,1)S(1)}, u32[]{:S(2)}, u32[]{:S(2)}) collective-permute-start(bf16[4,4,2,64,128]{4,3,2,1,0:T(8,128)(2,1)S(1)} %pad_maximum_fusion.1.refs_0_), channel_id=1, source_target_pairs={{32,0},{64,32},{96,64},{0,96},{33,1},{65,33},{97,65},{1,97},{34,2}... | collective-permute-start | bytes 1572872 | tf_op jit(solution)/shard_map/ppermute | solution.py:20
  139.9 24.8 %collective-permute-start.27 = (bf16[2,4,4,2,64,128]{5,4,3,2,1,0:T(8,128)(2,1)S(1)}, bf16[2,4,4,2,64,128]{5,4,3,2,1,0:T(8,128)(2,1)S(1)}, u32[]{:S(2)}, u32[]{:S(2)}) collective-permute-start(bf16[2,4,4,2,64,128]{5,4,3,2,1,0:T(8,128)(2,1)S(1)} %bitcast.149), channel_id=1, source_target_pairs={{32,0},{64,32},{96,64},{0,96},{33,1},{65,33},{97,65},{1,97},{34,2}... | collective-permute-start | bytes 3145736 | tf_op jit(solution)/shard_map/ppermute | solution.py:20
  142.2 28.4 %collective-permute-start.30 = (bf16[2,4,4,2,64,128]{5,4,3,2,1,0:T(8,128)(2,1)}, bf16[2,4,4,2,64,128]{5,4,3,2,1,0:T(8,128)(2,1)}, u32[]{:S(2)}, u32[]{:S(2)}) collective-permute-start(bf16[2,4,4,2,64,128]{5,4,3,2,1,0:T(8,128)(2,1)} %bitcast.46.refs_4_), channel_id=1, source_target_pairs={{2,0},{4,2},{6,4},{0,6},{3,1},{5,3},{7,5},{1,7},{10,8},{12,10},{14... | collective-permute-start | bytes 3145736 | tf_op jit(solution)/shard_map/ppermute | solution.py:20
  143.6 30.4 %collective-permute-start.24 = (bf16[32,8,1024]{2,1,0:T(8,128)(2,1)}, bf16[32,8,1024]{2,1,0:T(8,128)(2,1)}, u32[]{:S(2)}, u32[]{:S(2)}) collective-permute-start(bf16[32,8,1024]{2,1,0:T(8,128)(2,1)} %slice_select_fusion), channel_id=1, source_target_pairs={{31,0},{2,1},{1,2},{4,3},{3,4},{6,5},{5,6},{8,7},{7,8},{10,9},{9,1... | collective-permute-start | bytes 1572872 | tf_op jit(solution)/shard_map/ppermute | solution.py:30
  145.6 47.3 %collective-permute-start.29 = (bf16[2,4,4,2,64,128]{5,4,3,2,1,0:T(8,128)(2,1)S(1)}, bf16[2,4,4,2,64,128]{5,4,3,2,1,0:T(8,128)(2,1)S(1)}, u32[]{:S(2)}, u32[]{:S(2)}) collective-permute-start(bf16[2,4,4,2,64,128]{5,4,3,2,1,0:T(8,128)(2,1)S(1)} %bitcast.150), channel_id=1, source_target_pairs={{96,0},{0,32},{32,64},{64,96},{97,1},{1,33},{33,65},{65,97},{98,2}... | collective-permute-start | bytes 3145736 | tf_op jit(solution)/shard_map/ppermute | solution.py:20
  145.6 47.3 %collective-permute-start.32 = (bf16[2,4,4,2,64,128]{5,4,3,2,1,0:T(8,128)(2,1)}, bf16[2,4,4,2,64,128]{5,4,3,2,1,0:T(8,128)(2,1)}, u32[]{:S(2)}, u32[]{:S(2)}) collective-permute-start(bf16[2,4,4,2,64,128]{5,4,3,2,1,0:T(8,128)(2,1)} %bitcast.46.refs_4_), channel_id=1, source_target_pairs={{6,0},{0,2},{2,4},{4,6},{7,1},{1,3},{3,5},{5,7},{14,8},{8,10},{10,... | collective-permute-start | bytes 3145736 | tf_op jit(solution)/shard_map/ppermute | solution.py:20
  164.6 28.2 %collective-permute-start.28 = (bf16[2,4,4,2,64,128]{5,4,3,2,1,0:T(8,128)(2,1)S(1)}, bf16[2,4,4,2,64,128]{5,4,3,2,1,0:T(8,128)(2,1)}, u32[]{:S(2)}, u32[]{:S(2)}) collective-permute-start(bf16[2,4,4,2,64,128]{5,4,3,2,1,0:T(8,128)(2,1)S(1)} %collective-permute-done.27.refs_1_), channel_id=1, source_target_pairs={{32,0},{64,32},{96,64},{0,96},{33,1},{65,33},{97,65},{1,97},{34,2}... | collective-permute-start | bytes 3145736 | tf_op jit(solution)/shard_map/ppermute | solution.py:20
  170.6 25.3 %collective-permute-start.31 = (bf16[2,4,4,2,64,128]{5,4,3,2,1,0:T(8,128)(2,1)}, bf16[2,4,4,2,64,128]{5,4,3,2,1,0:T(8,128)(2,1)}, u32[]{:S(2)}, u32[]{:S(2)}) collective-permute-start(bf16[2,4,4,2,64,128]{5,4,3,2,1,0:T(8,128)(2,1)} %collective-permute-done.30.refs_5_), channel_id=1, source_target_pairs={{2,0},{4,2},{6,4},{0,6},{3,1},{5,3},{7,5},{1,7},{10,8},{12,10},{14... | collective-permute-start | bytes 3145736 | tf_op jit(solution)/shard_map/ppermute | solution.py:20
  178.0 9.0 %collective-permute-start.25 = (bf16[16,8,1024]{2,1,0:T(8,128)(2,1)}, bf16[16,8,1024]{2,1,0:T(8,128)(2,1)S(1)}, u32[]{:S(2)}, u32[]{:S(2)}) collective-permute-start(bf16[16,8,1024]{2,1,0:T(8,128)(2,1)} %slice.277), channel_id=1, source_target_pairs={{224,0},{0,32},{32,64},{64,96},{96,128},{128,160},{160,192},{192,2... | collective-permute-start | bytes 786440 | tf_op jit(solution)/shard_map/ppermute | solution.py:20
  190.7 5.2 %collective-permute-start.26 = (bf16[4,256,256]{2,1,0:T(8,128)(2,1)S(1)}, bf16[4,256,256]{2,1,0:T(8,128)(2,1)S(1)}, u32[]{:S(2)}, u32[]{:S(2)}) collective-permute-start(bf16[4,256,256]{2,1,0:T(8,128)(2,1)S(1)} %get-tuple-element.17.own), channel_id=1, source_target_pairs={{0,1},{1,0},{2,3},{3,2},{4,5},{5,4},{6,7},{7,6},{8,9},{9,8},{10,11... | collective-permute-start | bytes 1572872 | tf_op jit(solution)/shard_map/ppermute | solution.py:24
  (14 other events, 118.5 us)

commit v2 on v0

--- a/solution.py
+++ b/solution.py
@@ -115,35 +115,33 @@
     wide[384:] = jnp.concatenate(parts, 0).astype(BF16)
 
 
-def attn_kernel(pos, win, gain, *refs):
-    qk, vo, part, (xs, qs, ks, vs, att) = refs[:4], refs[4:8], refs[8], refs[9:]
+def stacked(block):
+    return jnp.concatenate(
+        [
+            jnp.concatenate([block(z, dy, a) for z in range(4) for dy in range(4)], 0)
+            for a in range(2)
+        ],
+        1,
+    )
+
+
+def score_kernel(pos, win, gain, *refs):
+    qk, xo, expo, (xs, qs, ks) = refs[:4], refs[4], refs[5], refs[6:]
     zhi, y = pos[2], pos[3]
     s = norm(win[...].astype(F32))
     for z in range(4):
         slab = to_relative(s[:, 256 * z : 256 * z + 256], y)
         xs[lax.rem(z + 4 - zhi, 4)] = slab.astype(BF16)
     x = jnp.concatenate([xs[i] for i in range(4)], 1)
+    xo[...] = x
     group = lax.broadcasted_iota(jnp.int32, (256, 256), 0) // HD
     mean = jnp.where(group == lax.broadcasted_iota(jnp.int32, (256, 256), 1) // HD, 1 / HD, 0.0)
     mean = mean.astype(BF16)
     lane = lax.broadcasted_iota(jnp.int32, (512, 128), 1)
-    ones = jnp.ones((256, 128), BF16)
     zero = jnp.zeros((512, 128), F32)
     for dx in range(4):
-
-        def stacked(block):
-            return jnp.concatenate(
-                [
-                    jnp.concatenate([block(z, dy, a) for z in range(4) for dy in range(4)], 0)
-                    for a in range(2)
-                ],
-                1,
-            )
-
         wqk = stacked(lambda z, dy, a: qk[dx][dy, z, a])
-        wvo = stacked(lambda z, dy, a: vo[dy][dx, z, a])
         pqk = jnp.dot(x, wqk, preferred_element_type=F32)
-        pv = jnp.dot(x, wvo, preferred_element_type=F32)
         square = pqk * pqk
         high = square.astype(BF16)
         low = (square - high.astype(F32)).astype(BF16)
@@ -155,17 +153,37 @@
             head = a * 4 + dx
             qs[head] = jnp.where(lane < HD, both * (HD**-0.5), zero).astype(BF16)
             ks[head] = pltpu.roll(both, HD, 1).astype(BF16)
-            v = pltpu.roll(pv[:, 128 * a : 128 * a + 128], HD, 1)
-            vs[head] = jnp.where(lane < HD, zero, v).astype(BF16)
 
     def heads(i, carry):
         for head in (2 * i, 2 * i + 1):
             for w in range(2):
                 t = slice(256 * w, 256 * w + 256)
                 score = lax.dot_general(qs[head, t], ks[head, t], NT, preferred_element_type=F32)
-                e = jnp.exp(score).astype(BF16)
+                expo[head, t] = jnp.exp(score).astype(BF16)
+        return carry
+
+    lax.fori_loop(0, 4, heads, 0)
+
+
+def value_kernel(pos, x, expo, *refs):
+    vo, part, (vs, att) = refs[:4], refs[4], refs[5:]
+    zhi, y = pos[2], pos[3]
+    lane = lax.broadcasted_iota(jnp.int32, (512, 128), 1)
+    ones = jnp.ones((256, 128), BF16)
+    zero = jnp.zeros((512, 128), F32)
+    for dx in range(4):
+        wvo = stacked(lambda z, dy, a: vo[dy][dx, z, a])
+        pv = jnp.dot(x[...], wvo, preferred_element_type=F32)
+        for a in range(2):
+            v = pltpu.roll(pv[:, 128 * a : 128 * a + 128], HD, 1)
+            vs[a * 4 + dx] = jnp.where(lane < HD, zero, v).astype(BF16)
+
+    def heads(i, carry):
+        for head in (2 * i, 2 * i + 1):
+            for w in range(2):
+                t = slice(256 * w, 256 * w + 256)
                 rhs = jnp.concatenate([vs[head, t], ones], 1)
-                o = jnp.dot(e, rhs, preferred_element_type=F32)
+                o = jnp.dot(expo[head, t], rhs, preferred_element_type=F32)
                 at = pl.multiple_of(128 * head, 128)
                 att[t, pl.ds(at, 128)] = (o[:, :128] / o[:, 128:]).astype(BF16)
         return carry
@@ -322,17 +340,24 @@
     mlp_x = ring4(mlp_x, "x")
     mlp_y = ring4(mlp_y, "y")
 
-    part = call(
-        attn_kernel,
-        sds((2 * count, width), BF16),
+    x, expo = call(
+        score_kernel,
+        (sds((2 * count, width), BF16), sds((8, 2 * count, 256), BF16)),
         pos,
         win,
         head_gain,
         *qk,
+        scratch=[pltpu.VMEM((4, 2 * count, 256), BF16)]
+        + [pltpu.VMEM((8, 2 * count, 128), BF16)] * 2,
+    )
+    part = call(
+        value_kernel,
+        sds((2 * count, width), BF16),
+        pos,
+        x,
+        expo,
         *vo,
-        scratch=[pltpu.VMEM((4, 2 * count, 256), BF16)]
-        + [pltpu.VMEM((8, 2 * count, 128), BF16)] * 3
-        + [pltpu.VMEM((2 * count, 1024), BF16)],
+        scratch=[pltpu.VMEM((8, 2 * count, 128), BF16), pltpu.VMEM((2 * count, 1024), BF16)],
     )
     full = (part.astype(F32) + swapped(part).astype(F32)).astype(BF16)
     full = full.reshape(rows, WIN, width)

time: 210 us -> 206 us (0.981)
  waiting for transfers between devices: 106 us -> 99.9 us
  Pallas kernels: 26.2 us -> 30.4 us
    ppermute x23, waiting for transfers between devices: 103 us -> 96.9 us  [from_offset(): return lax.ppermute(value, axis, [((i + offset) % n, i) for i in range(n)])]
    pallas_call x7 -> x8, Pallas kernels: 26.2 us -> 30.4 us  [call(): pl.pallas_call(kernel, out_shape=outs, in_specs=specs, out_specs=jax.tree...]
  transfers between devices with their start and end apart: 31 -> 31, of which waited for: 17 -> 16; matrix products, arithmetic and copies ran while one was open for 8% -> 8% of each run, Pallas kernels for 1% -> 5%
where the time goes in v2:
time: 206 us
  waiting for transfers between devices  99.9 us (48%)
  starting transfers between devices  48.2 us (23%)
  Pallas kernels  30.4 us (15%)
  local copies, waits for them, and re-layouts  15 us (7%)
  other arithmetic  7.06 us (3%)
  between operations  5.28 us (3%)
    ppermute x23, waiting for transfers between devices, from_offset(): return lax.ppermute(value, axis, [((i + offset) % n, i) for i in range(n)])  96.9 us
    ppermute x23, starting transfers between devices, from_offset(): return lax.ppermute(value, axis, [((i + offset) % n, i) for i in range(n)])  34.1 us
    pallas_call x8, Pallas kernels, call(): pl.pallas_call(kernel, out_shape=outs, in_specs=specs, out_specs=jax.tree...  30.4 us
    ppermute x6, starting transfers between devices, swapped(): return lax.ppermute(value, axis, [(0, 1), (1, 0)])  11.2 us
    unnamed x43, local copies, waits for them, and re-layouts  10.9 us
  transfers between devices with their start and end apart: 31, of which 16 were waited for; matrix products, arithmetic and copies ran while one was open for 8% of the time, Pallas kernels for 5%

profile of v2, /device:TPU:1, one launch (start us, length us, event | category | flops | bytes accessed | tf_op | source)
XLA Modules:
  0.0 205.9 jit_solution(8895333705782080172)
XLA Ops:
  3.7 3.3 %collective-permute-start.3 = (bf16[6,32,128]{2,1,0:T(8,128)(2,1)S(1)}, bf16[6,32,128]{2,1,0:T(8,128)(2,1)S(1)}, u32[]{:S(2)}, u32[]{:S(2)}) collective-permute-start(bf16[6,32,128]{2,1,0:T(8,128)(2,1)S(1)} %get-tuple-element.17), channel_id=1, source_target_pairs={{0,1},{1,0},{2,3},{3,2},{4,5},{5,4},{6,7},{7,6},{8,9},{9,8},{10,11... | collective-permute-start | bytes 147464 | tf_op jit(solution)/shard_map/ppermute | solution.py:24
  8.0 2.2 %collective-permute-start = (bf16[16,8,1024]{2,1,0:T(8,128)(2,1)S(1)}, bf16[16,8,1024]{2,1,0:T(8,128)(2,1)S(1)}, u32[]{:S(2)}, u32[]{:S(2)}) collective-permute-start(bf16[16,8,1024]{2,1,0:T(8,128)(2,1)S(1)} %slice.171), channel_id=1, source_target_pairs={{32,0},{64,32},{96,64},{128,96},{160,128},{192,160},{224,192},{0,2... | collective-permute-start | bytes 786440 | tf_op jit(solution)/shard_map/ppermute | solution.py:20
  18.7 3.1 %collective-permute-start.7 = (bf16[2,384,128]{2,1,0:T(8,128)(2,1)S(1)}, bf16[2,384,128]{2,1,0:T(8,128)(2,1)S(1)}, u32[]{:S(2)}, u32[]{:S(2)}) collective-permute-start(bf16[2,384,128]{2,1,0:T(8,128)(2,1)S(1)} %fusion.9), channel_id=1, source_target_pairs={{24,0},{0,8},{8,16},{16,24},{25,1},{1,9},{9,17},{17,25},{26,2},{2,... | collective-permute-start | bytes 589832 | tf_op jit(solution)/shard_map/ppermute | solution.py:20
  21.8 5.1 %collective-permute-start.6 = (bf16[2,384,128]{2,1,0:T(8,128)(2,1)S(1)}, bf16[2,384,128]{2,1,0:T(8,128)(2,1)S(1)}, u32[]{:S(2)}, u32[]{:S(2)}) collective-permute-start(bf16[2,384,128]{2,1,0:T(8,128)(2,1)S(1)} %fusion.9), channel_id=1, source_target_pairs={{16,0},{24,8},{0,16},{8,24},{17,1},{25,9},{1,17},{9,25},{18,2},{26... | collective-permute-start | bytes 589832 | tf_op jit(solution)/shard_map/ppermute | solution.py:20
  26.9 2.4 %collective-permute-start.5 = (bf16[2,384,128]{2,1,0:T(8,128)(2,1)S(1)}, bf16[2,384,128]{2,1,0:T(8,128)(2,1)S(1)}, u32[]{:S(2)}, u32[]{:S(2)}) collective-permute-start(bf16[2,384,128]{2,1,0:T(8,128)(2,1)S(1)} %fusion.9), channel_id=1, source_target_pairs={{8,0},{16,8},{24,16},{0,24},{9,1},{17,9},{25,17},{1,25},{10,2},{18... | collective-permute-start | bytes 589832 | tf_op jit(solution)/shard_map/ppermute | solution.py:20
  29.5 3.0 %collective-permute-start.1 = (bf16[32,8,1024]{2,1,0:T(8,128)(2,1)S(1)}, bf16[32,8,1024]{2,1,0:T(8,128)(2,1)S(1)}, u32[]{:S(2)}, u32[]{:S(2)}) collective-permute-start(bf16[32,8,1024]{2,1,0:T(8,128)(2,1)S(1)} %fusion.5), channel_id=1, source_target_pairs={{31,0},{2,1},{1,2},{4,3},{3,4},{6,5},{5,6},{8,7},{7,8},{10,9},{9,1... | collective-permute-start | bytes 1572872 | tf_op jit(solution)/shard_map/ppermute | solution.py:30
  32.5 5.3 %collective-permute-done.6 = bf16[2,384,128]{2,1,0:T(8,128)(2,1)S(1)} collective-permute-done((bf16[2,384,128]{2,1,0:T(8,128)(2,1)S(1)}, bf16[2,384,128]{2,1,0:T(8,128)(2,1)S(1)}, u32[]{:S(2)}, u32[]{:S(2)}) %collective-permute-start.6) | collective-permute-done | bytes 196640 | tf_op jit(solution)/shard_map/ppermute | solution.py:20
  37.8 13.3 %collective-permute-done.5 = bf16[2,384,128]{2,1,0:T(8,128)(2,1)S(1)} collective-permute-done((bf16[2,384,128]{2,1,0:T(8,128)(2,1)S(1)}, bf16[2,384,128]{2,1,0:T(8,128)(2,1)S(1)}, u32[]{:S(2)}, u32[]{:S(2)}) %collective-permute-start.5) | collective-permute-done | bytes 196640 | tf_op jit(solution)/shard_map/ppermute | solution.py:20
  51.4 2.6 %collective-permute-start.8 = (bf16[4,2,192,128]{3,2,1,0:T(8,128)(2,1)S(1)}, bf16[4,2,192,128]{3,2,1,0:T(8,128)(2,1)S(1)}, u32[]{:S(2)}, u32[]{:S(2)}) collective-permute-start(bf16[4,2,192,128]{3,2,1,0:T(8,128)(2,1)S(1)} %pad_maximum_fusion.3), channel_id=1, source_target_pairs={{2,0},{4,2},{6,4},{0,6},{3,1},{5,3},{7,5},{1,7},{10,8},{12,10},{14... | collective-permute-start | bytes 1179656 | tf_op jit(solution)/shard_map/ppermute | solution.py:20
  54.9 16.2 %collective-permute-done.10 = bf16[4,2,192,128]{3,2,1,0:T(8,128)(2,1)S(1)} collective-permute-done((bf16[4,2,192,128]{3,2,1,0:T(8,128)(2,1)S(1)}, bf16[4,2,192,128]{3,2,1,0:T(8,128)(2,1)S(1)}, u32[]{:S(2)}, u32[]{:S(2)}) %collective-permute-start.10) | collective-permute-done | bytes 393248 | tf_op jit(solution)/shard_map/ppermute | solution.py:20
  73.1 3.1 %collective-permute-start.15 = (bf16[4,4,2,64,128]{4,3,2,1,0:T(8,128)(2,1)S(1)}, bf16[4,4,2,64,128]{4,3,2,1,0:T(8,128)(2,1)S(1)}, u32[]{:S(2)}, u32[]{:S(2)}) collective-permute-start(bf16[4,4,2,64,128]{4,3,2,1,0:T(8,128)(2,1)S(1)} %pad_maximum_fusion.1.refs_0_), channel_id=1, source_target_pairs={{64,0},{96,32},{0,64},{32,96},{65,1},{97,33},{1,65},{33,97},{66,2}... | collective-permute-start | bytes 1572872 | tf_op jit(solution)/shard_map/ppermute | solution.py:20
  76.1 6.2 %collective-permute-done.12 = bf16[1600,128]{1,0:T(8,128)(2,1)S(1)} collective-permute-done((bf16[1600,128]{1,0:T(8,128)(2,1)S(1)}, bf16[1600,128]{1,0:T(8,128)(2,1)S(1)}, u32[]{:S(2)}, u32[]{:S(2)}) %collective-permute-start.12) | collective-permute-done | bytes 409632 | tf_op jit(solution)/shard_map/ppermute | solution.py:20
  82.3 6.6 %collective-permute-done.11 = bf16[1600,128]{1,0:T(8,128)(2,1)S(1)} collective-permute-done((bf16[1600,128]{1,0:T(8,128)(2,1)S(1)}, bf16[1600,128]{1,0:T(8,128)(2,1)S(1)}, u32[]{:S(2)}, u32[]{:S(2)}) %collective-permute-start.11) | collective-permute-done | bytes 409632 | tf_op jit(solution)/shard_map/ppermute | solution.py:20
  90.9 2.3 %collective-permute-start.2 = (bf16[2,32,8,1024]{3,2,1,0:T(8,128)(2,1)S(1)}, bf16[2,32,8,1024]{3,2,1,0:T(8,128)(2,1)S(1)}, u32[]{:S(2)}, u32[]{:S(2)}) collective-permute-start(bf16[2,32,8,1024]{3,2,1,0:T(8,128)(2,1)S(1)} %pad_maximum_fusion), channel_id=1, source_target_pairs={{0,1},{1,0},{2,3},{3,2},{4,5},{5,4},{6,7},{7,6},{8,9},{9,8},{10,11... | collective-permute-start | bytes 3145736 | tf_op jit(solution)/shard_map/ppermute | solution.py:24
  101.7 3.1 %collective-permute-done.15.refs_2_ = bf16[4,4,2,64,128]{4,3,2,1,0:T(8,128)(2,1)S(1)} collective-permute-done((bf16[4,4,2,64,128]{4,3,2,1,0:T(8,128)(2,1)S(1)}, bf16[4,4,2,64,128]{4,3,2,1,0:T(8,128)(2,1)S(1)}, u32[]{:S(2)}, u32[]{:S(2)}) %collective-permute-start.15) | collective-permute-done | bytes 524320 | tf_op jit(solution)/shard_map/ppermute | solution.py:20
  104.8 5.4 %collective-permute-done.14.refs_1_ = bf16[4,4,2,64,128]{4,3,2,1,0:T(8,128)(2,1)S(1)} collective-permute-done((bf16[4,4,2,64,128]{4,3,2,1,0:T(8,128)(2,1)S(1)}, bf16[4,4,2,64,128]{4,3,2,1,0:T(8,128)(2,1)S(1)}, u32[]{:S(2)}, u32[]{:S(2)}) %collective-permute-start.14) | collective-permute-done | bytes 524320 | tf_op jit(solution)/shard_map/ppermute | solution.py:20
  110.2 7.4 %shard_map.102 = (bf16[512,1024]{1,0:T(8,128)(2,1)S(1)}, bf16[8,512,256]{2,1,0:T(8,128)(2,1)}) custom-call(s32[4]{0:T(128)S(1)} %pad_add_fusion.pos, bf16[512,1024]{1,0:T(8,128)(2,1)S(1)} %bitcast.147, f32[8,128]{1,0:T(8,128)S(1)} %bitcast.156, bf16[4,4,2,64,128]{4,3,2,1,0:T(8,128)(2,1)S(1)} %pad_maximum_fusion.1.refs_0_, ...), custom_call_target="tpu_custom_call" | custom-call | tf_op jit(solution)/shard_map/pallas_call | solution.py:48
  117.6 5.6 %collective-permute-done.17.refs_1_ = bf16[4,4,2,64,128]{4,3,2,1,0:T(8,128)(2,1)S(1)} collective-permute-done((bf16[4,4,2,64,128]{4,3,2,1,0:T(8,128)(2,1)S(1)}, bf16[4,4,2,64,128]{4,3,2,1,0:T(8,128)(2,1)S(1)}, u32[]{:S(2)}, u32[]{:S(2)}) %collective-permute-start.17) | collective-permute-done | bytes 524320 | tf_op jit(solution)/shard_map/ppermute | solution.py:20
  123.2 6.4 %shard_map.103 = bf16[512,1024]{1,0:T(8,128)(2,1)S(1)} custom-call(s32[4]{0:T(128)S(1)} %pad_add_fusion.pos, bf16[512,1024]{1,0:T(8,128)(2,1)S(1)} %get-tuple-element.19.x, bf16[8,512,256]{2,1,0:T(8,128)(2,1)} %get-tuple-element.20.expo, bf16[4,4,2,64,128]{4,3,2,1,0:T(8,128)(2,1)S(1)} %pad_maximum_fusion.2.refs_0_, ...), custom_call_target="tpu_custom_call" | custom-call | tf_op jit(solution)/shard_map/pallas_call | solution.py:48
  130.5 2.5 %collective-permute-start.24 = (bf16[2,4,4,2,64,128]{5,4,3,2,1,0:T(8,128)(2,1)S(1)}, bf16[2,4,4,2,64,128]{5,4,3,2,1,0:T(8,128)(2,1)S(1)}, u32[]{:S(2)}, u32[]{:S(2)}) collective-permute-start(bf16[2,4,4,2,64,128]{5,4,3,2,1,0:T(8,128)(2,1)S(1)} %bitcast.143), channel_id=1, source_target_pairs={{32,0},{64,32},{96,64},{0,96},{33,1},{65,33},{97,65},{1,97},{34,2}... | collective-permute-start | bytes 3145736 | tf_op jit(solution)/shard_map/ppermute | solution.py:20
  133.0 2.1 %collective-permute-start.27 = (bf16[2,4,4,2,64,128]{5,4,3,2,1,0:T(8,128)(2,1)}, bf16[2,4,4,2,64,128]{5,4,3,2,1,0:T(8,128)(2,1)}, u32[]{:S(2)}, u32[]{:S(2)}) collective-permute-start(bf16[2,4,4,2,64,128]{5,4,3,2,1,0:T(8,128)(2,1)} %bitcast.51.refs_4_), channel_id=1, source_target_pairs={{2,0},{4,2},{6,4},{0,6},{3,1},{5,3},{7,5},{1,7},{10,8},{12,10},{14... | collective-permute-start | bytes 3145736 | tf_op jit(solution)/shard_map/ppermute | solution.py:20
  136.6 18.8 %collective-permute-done.24.refs_1_ = bf16[2,4,4,2,64,128]{5,4,3,2,1,0:T(8,128)(2,1)S(1)} collective-permute-done((bf16[2,4,4,2,64,128]{5,4,3,2,1,0:T(8,128)(2,1)S(1)}, bf16[2,4,4,2,64,128]{5,4,3,2,1,0:T(8,128)(2,1)S(1)}, u32[]{:S(2)}, u32[]{:S(2)}) %collective-permute-start.24) | collective-permute-done | bytes 1048608 | tf_op jit(solution)/shard_map/ppermute | solution.py:20
  155.4 3.5 %collective-permute-start.25 = (bf16[2,4,4,2,64,128]{5,4,3,2,1,0:T(8,128)(2,1)S(1)}, bf16[2,4,4,2,64,128]{5,4,3,2,1,0:T(8,128)(2,1)}, u32[]{:S(2)}, u32[]{:S(2)}) collective-permute-start(bf16[2,4,4,2,64,128]{5,4,3,2,1,0:T(8,128)(2,1)S(1)} %collective-permute-done.24.refs_1_), channel_id=1, source_target_pairs={{32,0},{64,32},{96,64},{0,96},{33,1},{65,33},{97,65},{1,97},{34,2}... | collective-permute-start | bytes 3145736 | tf_op jit(solution)/shard_map/ppermute | solution.py:20
  158.9 4.3 %collective-permute-done.27.refs_5_ = bf16[2,4,4,2,64,128]{5,4,3,2,1,0:T(8,128)(2,1)} collective-permute-done((bf16[2,4,4,2,64,128]{5,4,3,2,1,0:T(8,128)(2,1)}, bf16[2,4,4,2,64,128]{5,4,3,2,1,0:T(8,128)(2,1)}, u32[]{:S(2)}, u32[]{:S(2)}) %collective-permute-start.27) | collective-permute-done | bytes 1048608 | tf_op jit(solution)/shard_map/ppermute | solution.py:20
  163.2 3.4 %collective-permute-start.28 = (bf16[2,4,4,2,64,128]{5,4,3,2,1,0:T(8,128)(2,1)}, bf16[2,4,4,2,64,128]{5,4,3,2,1,0:T(8,128)(2,1)}, u32[]{:S(2)}, u32[]{:S(2)}) collective-permute-start(bf16[2,4,4,2,64,128]{5,4,3,2,1,0:T(8,128)(2,1)} %collective-permute-done.27.refs_5_), channel_id=1, source_target_pairs={{2,0},{4,2},{6,4},{0,6},{3,1},{5,3},{7,5},{1,7},{10,8},{12,10},{14... | collective-permute-start | bytes 3145736 | tf_op jit(solution)/shard_map/ppermute | solution.py:20
  166.6 2.6 %fusion.7 = bf16[32,8,1024]{2,1,0:T(8,128)(2,1)S(1)} fusion(s32[]{:T(128)S(6)} %select_n.54, bf16[32,16,1024]{2,1,0:T(8,128)(2,1)} %bitcast.163, bf16[32,8,1024]{2,1,0:T(8,128)(2,1)} %collective-permute-done.21, pred[]{:T(512)S(6)} %eq.3), kind=kLoop, calls=%fused_computation.23 | loop fusion | flops 2359296 | bytes 2097157 | tf_op jit(solution)/shard_map/jit(_where)/select_n | solution.py:366
  171.9 7.5 %collective-permute-done.22 = bf16[16,8,1024]{2,1,0:T(8,128)(2,1)S(1)} collective-permute-done((bf16[16,8,1024]{2,1,0:T(8,128)(2,1)}, bf16[16,8,1024]{2,1,0:T(8,128)(2,1)S(1)}, u32[]{:S(2)}, u32[]{:S(2)}) %collective-permute-start.22) | collective-permute-done | bytes 262176 | tf_op jit(solution)/shard_map/ppermute | solution.py:20
  183.1 2.5 %collective-permute-start.23 = (bf16[4,256,256]{2,1,0:T(8,128)(2,1)S(1)}, bf16[4,256,256]{2,1,0:T(8,128)(2,1)S(1)}, u32[]{:S(2)}, u32[]{:S(2)}) collective-permute-start(bf16[4,256,256]{2,1,0:T(8,128)(2,1)S(1)} %get-tuple-element.21.own), channel_id=1, source_target_pairs={{0,1},{1,0},{2,3},{3,2},{4,5},{5,4},{6,7},{7,6},{8,9},{9,8},{10,11... | collective-permute-start | bytes 1572872 | tf_op jit(solution)/shard_map/ppermute | solution.py:24
  185.6 2.6 %collective-permute-done.28.refs_6_ = bf16[2,4,4,2,64,128]{5,4,3,2,1,0:T(8,128)(2,1)} collective-permute-done((bf16[2,4,4,2,64,128]{5,4,3,2,1,0:T(8,128)(2,1)}, bf16[2,4,4,2,64,128]{5,4,3,2,1,0:T(8,128)(2,1)}, u32[]{:S(2)}, u32[]{:S(2)}) %collective-permute-start.28) | collective-permute-done | bytes 1048608 | tf_op jit(solution)/shard_map/ppermute | solution.py:20
  188.2 6.4 %shard_map.105.act = bf16[512,2048]{1,0:T(8,128)(2,1)} custom-call(s32[4]{0:T(128)S(1)} %pad_add_fusion.pos, bf16[4,256,256]{2,1,0:T(8,128)(2,1)S(1)} %get-tuple-element.21.own, bf16[4,256,256]{2,1,0:T(8,128)(2,1)S(1)} %collective-permute-done.23.other, f32[8,256]{1,0:T(8,128)S(1)} %bitcast.153, bf16[2,4,4,2,64,128]{5,4,3,2,1,0:T(8,128)(2,1)S(1)} %bitcast.145, ...), custom_call_target="tpu_custom_call" | custom-call | tf_op jit(solution)/shard_map/pallas_call | solution.py:48
  194.6 5.6 %shard_map.106 = (f32[256,1024]{1,0:T(8,128)S(1)}, bf16[256,1024]{1,0:T(8,128)(2,1)S(1)}) custom-call(s32[4]{0:T(128)S(1)} %pad_add_fusion.pos, bf16[512,2048]{1,0:T(8,128)(2,1)} %shard_map.105.act, bf16[2,4,4,2,64,128]{5,4,3,2,1,0:T(8,128)(2,1)S(1)} %bitcast.146, bf16[2,4,4,2,64,128]{5,4,3,2,1,0:T(8,128)(2,1)S(1)} %collective-permute-done.24.refs_1_, ...), custom_call_target="tpu_custom_call" | custom-call | tf_op jit(solution)/shard_map/pallas_call | solution.py:48
  200.3 2.2 %collective-permute-start.30 = (bf16[256,1024]{1,0:T(8,128)(2,1)S(1)}, bf16[256,1024]{1,0:T(8,128)(2,1)S(1)}, u32[]{:S(2)}, u32[]{:S(2)}) collective-permute-start(bf16[256,1024]{1,0:T(8,128)(2,1)S(1)} %get-tuple-element.25), channel_id=1, source_target_pairs={{0,1},{1,0},{2,3},{3,2},{4,5},{5,4},{6,7},{7,6},{8,9},{9,8},{10,11... | collective-permute-start | bytes 1572872 | tf_op jit(solution)/shard_map/ppermute | solution.py:24
  (125 shorter events, 34.3 us)
Async XLA Ops:
  3.7 6.5 %collective-permute-start.3 = (bf16[6,32,128]{2,1,0:T(8,128)(2,1)S(1)}, bf16[6,32,128]{2,1,0:T(8,128)(2,1)S(1)}, u32[]{:S(2)}, u32[]{:S(2)}) collective-permute-start(bf16[6,32,128]{2,1,0:T(8,128)(2,1)S(1)} %get-tuple-element.17), channel_id=1, source_target_pairs={{0,1},{1,0},{2,3},{3,2},{4,5},{5,4},{6,7},{7,6},{8,9},{9,8},{10,11... | collective-permute-start | bytes 147464 | tf_op jit(solution)/shard_map/ppermute | solution.py:24
  8.0 21.3 %collective-permute-start = (bf16[16,8,1024]{2,1,0:T(8,128)(2,1)S(1)}, bf16[16,8,1024]{2,1,0:T(8,128)(2,1)S(1)}, u32[]{:S(2)}, u32[]{:S(2)}) collective-permute-start(bf16[16,8,1024]{2,1,0:T(8,128)(2,1)S(1)} %slice.171), channel_id=1, source_target_pairs={{32,0},{64,32},{96,64},{128,96},{160,128},{192,160},{224,192},{0,2... | collective-permute-start | bytes 786440 | tf_op jit(solution)/shard_map/ppermute | solution.py:20
  12.1 6.5 %collective-permute-start.4 = (bf16[416,128]{1,0:T(8,128)(2,1)S(1)}, bf16[416,128]{1,0:T(8,128)(2,1)S(1)}, u32[]{:S(2)}, u32[]{:S(2)}) collective-permute-start(bf16[416,128]{1,0:T(8,128)(2,1)S(1)} %shard_map.101), channel_id=1, source_target_pairs={{0,128},{128,0},{1,129},{129,1},{2,130},{130,2},{3,131},{131,3},{4... | collective-permute-start | bytes 319496 | tf_op jit(solution)/shard_map/ppermute | solution.py:24
  18.7 13.8 %collective-permute-start.7 = (bf16[2,384,128]{2,1,0:T(8,128)(2,1)S(1)}, bf16[2,384,128]{2,1,0:T(8,128)(2,1)S(1)}, u32[]{:S(2)}, u32[]{:S(2)}) collective-permute-start(bf16[2,384,128]{2,1,0:T(8,128)(2,1)S(1)} %fusion.9), channel_id=1, source_target_pairs={{24,0},{0,8},{8,16},{16,24},{25,1},{1,9},{9,17},{17,25},{26,2},{2,... | collective-permute-start | bytes 589832 | tf_op jit(solution)/shard_map/ppermute | solution.py:20
  21.8 16.0 %collective-permute-start.6 = (bf16[2,384,128]{2,1,0:T(8,128)(2,1)S(1)}, bf16[2,384,128]{2,1,0:T(8,128)(2,1)S(1)}, u32[]{:S(2)}, u32[]{:S(2)}) collective-permute-start(bf16[2,384,128]{2,1,0:T(8,128)(2,1)S(1)} %fusion.9), channel_id=1, source_target_pairs={{16,0},{24,8},{0,16},{8,24},{17,1},{25,9},{1,17},{9,25},{18,2},{26... | collective-permute-start | bytes 589832 | tf_op jit(solution)/shard_map/ppermute | solution.py:20
  26.9 24.2 %collective-permute-start.5 = (bf16[2,384,128]{2,1,0:T(8,128)(2,1)S(1)}, bf16[2,384,128]{2,1,0:T(8,128)(2,1)S(1)}, u32[]{:S(2)}, u32[]{:S(2)}) collective-permute-start(bf16[2,384,128]{2,1,0:T(8,128)(2,1)S(1)} %fusion.9), channel_id=1, source_target_pairs={{8,0},{16,8},{24,16},{0,24},{9,1},{17,9},{25,17},{1,25},{10,2},{18... | collective-permute-start | bytes 589832 | tf_op jit(solution)/shard_map/ppermute | solution.py:20
  29.5 61.2 %collective-permute-start.1 = (bf16[32,8,1024]{2,1,0:T(8,128)(2,1)S(1)}, bf16[32,8,1024]{2,1,0:T(8,128)(2,1)S(1)}, u32[]{:S(2)}, u32[]{:S(2)}) collective-permute-start(bf16[32,8,1024]{2,1,0:T(8,128)(2,1)S(1)} %fusion.5), channel_id=1, source_target_pairs={{31,0},{2,1},{1,2},{4,3},{3,4},{6,5},{5,6},{8,7},{7,8},{10,9},{9,1... | collective-permute-start | bytes 1572872 | tf_op jit(solution)/shard_map/ppermute | solution.py:30
  51.2 19.9 %collective-permute-start.10 = (bf16[4,2,192,128]{3,2,1,0:T(8,128)(2,1)S(1)}, bf16[4,2,192,128]{3,2,1,0:T(8,128)(2,1)S(1)}, u32[]{:S(2)}, u32[]{:S(2)}) collective-permute-start(bf16[4,2,192,128]{3,2,1,0:T(8,128)(2,1)S(1)} %pad_maximum_fusion.3), channel_id=1, source_target_pairs={{6,0},{0,2},{2,4},{4,6},{7,1},{1,3},{3,5},{5,7},{14,8},{8,10},{10,... | collective-permute-start | bytes 1179656 | tf_op jit(solution)/shard_map/ppermute | solution.py:20
  51.3 19.8 %collective-permute-start.9 = (bf16[4,2,192,128]{3,2,1,0:T(8,128)(2,1)S(1)}, bf16[4,2,192,128]{3,2,1,0:T(8,128)(2,1)S(1)}, u32[]{:S(2)}, u32[]{:S(2)}) collective-permute-start(bf16[4,2,192,128]{3,2,1,0:T(8,128)(2,1)S(1)} %pad_maximum_fusion.3), channel_id=1, source_target_pairs={{4,0},{6,2},{0,4},{2,6},{5,1},{7,3},{1,5},{3,7},{12,8},{14,10},{8,... | collective-permute-start | bytes 1179656 | tf_op jit(solution)/shard_map/ppermute | solution.py:20
  51.4 21.2 %collective-permute-start.8 = (bf16[4,2,192,128]{3,2,1,0:T(8,128)(2,1)S(1)}, bf16[4,2,192,128]{3,2,1,0:T(8,128)(2,1)S(1)}, u32[]{:S(2)}, u32[]{:S(2)}) collective-permute-start(bf16[4,2,192,128]{3,2,1,0:T(8,128)(2,1)S(1)} %pad_maximum_fusion.3), channel_id=1, source_target_pairs={{2,0},{4,2},{6,4},{0,6},{3,1},{5,3},{7,5},{1,7},{10,8},{12,10},{14... | collective-permute-start | bytes 1179656 | tf_op jit(solution)/shard_map/ppermute | solution.py:20
  54.1 19.0 %collective-permute-start.13 = (bf16[1600,128]{1,0:T(8,128)(2,1)S(1)}, bf16[1600,128]{1,0:T(8,128)(2,1)S(1)}, u32[]{:S(2)}, u32[]{:S(2)}) collective-permute-start(bf16[1600,128]{1,0:T(8,128)(2,1)S(1)} %constant_dynamic-update-slice_fusion), channel_id=1, source_target_pairs={{96,0},{0,32},{32,64},{64,96},{97,1},{1,33},{33,65},{65,97},{98,2}... | collective-permute-start | bytes 1228808 | tf_op jit(solution)/shard_map/ppermute | solution.py:20
  71.1 11.2 %collective-permute-start.12 = (bf16[1600,128]{1,0:T(8,128)(2,1)S(1)}, bf16[1600,128]{1,0:T(8,128)(2,1)S(1)}, u32[]{:S(2)}, u32[]{:S(2)}) collective-permute-start(bf16[1600,128]{1,0:T(8,128)(2,1)S(1)} %constant_dynamic-update-slice_fusion), channel_id=1, source_target_pairs={{64,0},{96,32},{0,64},{32,96},{65,1},{97,33},{1,65},{33,97},{66,2}... | collective-permute-start | bytes 1228808 | tf_op jit(solution)/shard_map/ppermute | solution.py:20
  71.1 17.8 %collective-permute-start.11 = (bf16[1600,128]{1,0:T(8,128)(2,1)S(1)}, bf16[1600,128]{1,0:T(8,128)(2,1)S(1)}, u32[]{:S(2)}, u32[]{:S(2)}) collective-permute-start(bf16[1600,128]{1,0:T(8,128)(2,1)S(1)} %constant_dynamic-update-slice_fusion), channel_id=1, source_target_pairs={{32,0},{64,32},{96,64},{0,96},{33,1},{65,33},{97,65},{1,97},{34,2}... | collective-permute-start | bytes 1228808 | tf_op jit(solution)/shard_map/ppermute | solution.py:20
  72.7 24.2 %collective-permute-start.16 = (bf16[4,4,2,64,128]{4,3,2,1,0:T(8,128)(2,1)S(1)}, bf16[4,4,2,64,128]{4,3,2,1,0:T(8,128)(2,1)S(1)}, u32[]{:S(2)}, u32[]{:S(2)}) collective-permute-start(bf16[4,4,2,64,128]{4,3,2,1,0:T(8,128)(2,1)S(1)} %pad_maximum_fusion.1.refs_0_), channel_id=1, source_target_pairs={{96,0},{0,32},{32,64},{64,96},{97,1},{1,33},{33,65},{65,97},{98,2}... | collective-permute-start | bytes 1572872 | tf_op jit(solution)/shard_map/ppermute | solution.py:20
  73.1 31.7 %collective-permute-start.15 = (bf16[4,4,2,64,128]{4,3,2,1,0:T(8,128)(2,1)S(1)}, bf16[4,4,2,64,128]{4,3,2,1,0:T(8,128)(2,1)S(1)}, u32[]{:S(2)}, u32[]{:S(2)}) collective-permute-start(bf16[4,4,2,64,128]{4,3,2,1,0:T(8,128)(2,1)S(1)} %pad_maximum_fusion.1.refs_0_), channel_id=1, source_target_pairs={{64,0},{96,32},{0,64},{32,96},{65,1},{97,33},{1,65},{33,97},{66,2}... | collective-permute-start | bytes 1572872 | tf_op jit(solution)/shard_map/ppermute | solution.py:20
  82.3 27.9 %collective-permute-start.14 = (bf16[4,4,2,64,128]{4,3,2,1,0:T(8,128)(2,1)S(1)}, bf16[4,4,2,64,128]{4,3,2,1,0:T(8,128)(2,1)S(1)}, u32[]{:S(2)}, u32[]{:S(2)}) collective-permute-start(bf16[4,4,2,64,128]{4,3,2,1,0:T(8,128)(2,1)S(1)} %pad_maximum_fusion.1.refs_0_), channel_id=1, source_target_pairs={{32,0},{64,32},{96,64},{0,96},{33,1},{65,33},{97,65},{1,97},{34,2}... | collective-permute-start | bytes 1572872 | tf_op jit(solution)/shard_map/ppermute | solution.py:20
  89.2 28.4 %collective-permute-start.19 = (bf16[4,4,2,64,128]{4,3,2,1,0:T(8,128)(2,1)S(1)}, bf16[4,4,2,64,128]{4,3,2,1,0:T(8,128)(2,1)S(1)}, u32[]{:S(2)}, u32[]{:S(2)}) collective-permute-start(bf16[4,4,2,64,128]{4,3,2,1,0:T(8,128)(2,1)S(1)} %pad_maximum_fusion.2.refs_0_), channel_id=1, source_target_pairs={{6,0},{0,2},{2,4},{4,6},{7,1},{1,3},{3,5},{5,7},{14,8},{8,10},{10,... | collective-permute-start | bytes 1572872 | tf_op jit(solution)/shard_map/ppermute | solution.py:20
  90.9 8.1 %collective-permute-start.2 = (bf16[2,32,8,1024]{3,2,1,0:T(8,128)(2,1)S(1)}, bf16[2,32,8,1024]{3,2,1,0:T(8,128)(2,1)S(1)}, u32[]{:S(2)}, u32[]{:S(2)}) collective-permute-start(bf16[2,32,8,1024]{3,2,1,0:T(8,128)(2,1)S(1)} %pad_maximum_fusion), channel_id=1, source_target_pairs={{0,1},{1,0},{2,3},{3,2},{4,5},{5,4},{6,7},{7,6},{8,9},{9,8},{10,11... | collective-permute-start | bytes 3145736 | tf_op jit(solution)/shard_map/ppermute | solution.py:24
  96.9 20.7 %collective-permute-start.18 = (bf16[4,4,2,64,128]{4,3,2,1,0:T(8,128)(2,1)S(1)}, bf16[4,4,2,64,128]{4,3,2,1,0:T(8,128)(2,1)S(1)}, u32[]{:S(2)}, u32[]{:S(2)}) collective-permute-start(bf16[4,4,2,64,128]{4,3,2,1,0:T(8,128)(2,1)S(1)} %pad_maximum_fusion.2.refs_0_), channel_id=1, source_target_pairs={{4,0},{6,2},{0,4},{2,6},{5,1},{7,3},{1,5},{3,7},{12,8},{14,10},{8,... | collective-permute-start | bytes 1572872 | tf_op jit(solution)/shard_map/ppermute | solution.py:20
  98.9 24.3 %collective-permute-start.17 = (bf16[4,4,2,64,128]{4,3,2,1,0:T(8,128)(2,1)S(1)}, bf16[4,4,2,64,128]{4,3,2,1,0:T(8,128)(2,1)S(1)}, u32[]{:S(2)}, u32[]{:S(2)}) collective-permute-start(bf16[4,4,2,64,128]{4,3,2,1,0:T(8,128)(2,1)S(1)} %pad_maximum_fusion.2.refs_0_), channel_id=1, source_target_pairs={{2,0},{4,2},{6,4},{0,6},{3,1},{5,3},{7,5},{1,7},{10,8},{12,10},{14... | collective-permute-start | bytes 1572872 | tf_op jit(solution)/shard_map/ppermute | solution.py:20
  129.6 5.6 %collective-permute-start.20 = (bf16[512,1024]{1,0:T(8,128)(2,1)S(1)}, bf16[512,1024]{1,0:T(8,128)(2,1)S(1)}, u32[]{:S(2)}, u32[]{:S(2)}) collective-permute-start(bf16[512,1024]{1,0:T(8,128)(2,1)S(1)} %shard_map.103), channel_id=1, source_target_pairs={{0,1},{1,0},{2,3},{3,2},{4,5},{5,4},{6,7},{7,6},{8,9},{9,8},{10,11... | collective-permute-start | bytes 3145736 | tf_op jit(solution)/shard_map/ppermute | solution.py:24
  130.5 24.9 %collective-permute-start.24 = (bf16[2,4,4,2,64,128]{5,4,3,2,1,0:T(8,128)(2,1)S(1)}, bf16[2,4,4,2,64,128]{5,4,3,2,1,0:T(8,128)(2,1)S(1)}, u32[]{:S(2)}, u32[]{:S(2)}) collective-permute-start(bf16[2,4,4,2,64,128]{5,4,3,2,1,0:T(8,128)(2,1)S(1)} %bitcast.143), channel_id=1, source_target_pairs={{32,0},{64,32},{96,64},{0,96},{33,1},{65,33},{97,65},{1,97},{34,2}... | collective-permute-start | bytes 3145736 | tf_op jit(solution)/shard_map/ppermute | solution.py:20
  133.0 30.2 %collective-permute-start.27 = (bf16[2,4,4,2,64,128]{5,4,3,2,1,0:T(8,128)(2,1)}, bf16[2,4,4,2,64,128]{5,4,3,2,1,0:T(8,128)(2,1)}, u32[]{:S(2)}, u32[]{:S(2)}) collective-permute-start(bf16[2,4,4,2,64,128]{5,4,3,2,1,0:T(8,128)(2,1)} %bitcast.51.refs_4_), channel_id=1, source_target_pairs={{2,0},{4,2},{6,4},{0,6},{3,1},{5,3},{7,5},{1,7},{10,8},{12,10},{14... | collective-permute-start | bytes 3145736 | tf_op jit(solution)/shard_map/ppermute | solution.py:20
  136.5 44.0 %copy-start.6 = (f32[1024]{0:T(1024)S(1)}, f32[1024]{0:T(1024)}, u32[]{:S(2)}) copy-start(f32[1024]{0:T(1024)} %param.17) | copy-start | bytes 12292
  136.5 30.1 %collective-permute-start.21 = (bf16[32,8,1024]{2,1,0:T(8,128)(2,1)}, bf16[32,8,1024]{2,1,0:T(8,128)(2,1)}, u32[]{:S(2)}, u32[]{:S(2)}) collective-permute-start(bf16[32,8,1024]{2,1,0:T(8,128)(2,1)} %slice_select_fusion), channel_id=1, source_target_pairs={{31,0},{2,1},{1,2},{4,3},{3,4},{6,5},{5,6},{8,7},{7,8},{10,9},{9,1... | collective-permute-start | bytes 1572872 | tf_op jit(solution)/shard_map/ppermute | solution.py:30
  136.5 49.0 %collective-permute-start.26 = (bf16[2,4,4,2,64,128]{5,4,3,2,1,0:T(8,128)(2,1)S(1)}, bf16[2,4,4,2,64,128]{5,4,3,2,1,0:T(8,128)(2,1)S(1)}, u32[]{:S(2)}, u32[]{:S(2)}) collective-permute-start(bf16[2,4,4,2,64,128]{5,4,3,2,1,0:T(8,128)(2,1)S(1)} %bitcast.144), channel_id=1, source_target_pairs={{96,0},{0,32},{32,64},{64,96},{97,1},{1,33},{33,65},{65,97},{98,2}... | collective-permute-start | bytes 3145736 | tf_op jit(solution)/shard_map/ppermute | solution.py:20
  136.5 49.0 %collective-permute-start.29 = (bf16[2,4,4,2,64,128]{5,4,3,2,1,0:T(8,128)(2,1)}, bf16[2,4,4,2,64,128]{5,4,3,2,1,0:T(8,128)(2,1)}, u32[]{:S(2)}, u32[]{:S(2)}) collective-permute-start(bf16[2,4,4,2,64,128]{5,4,3,2,1,0:T(8,128)(2,1)} %bitcast.51.refs_4_), channel_id=1, source_target_pairs={{6,0},{0,2},{2,4},{4,6},{7,1},{1,3},{3,5},{5,7},{14,8},{8,10},{10,... | collective-permute-start | bytes 3145736 | tf_op jit(solution)/shard_map/ppermute | solution.py:20
  155.4 30.2 %collective-permute-start.25 = (bf16[2,4,4,2,64,128]{5,4,3,2,1,0:T(8,128)(2,1)S(1)}, bf16[2,4,4,2,64,128]{5,4,3,2,1,0:T(8,128)(2,1)}, u32[]{:S(2)}, u32[]{:S(2)}) collective-permute-start(bf16[2,4,4,2,64,128]{5,4,3,2,1,0:T(8,128)(2,1)S(1)} %collective-permute-done.24.refs_1_), channel_id=1, source_target_pairs={{32,0},{64,32},{96,64},{0,96},{33,1},{65,33},{97,65},{1,97},{34,2}... | collective-permute-start | bytes 3145736 | tf_op jit(solution)/shard_map/ppermute | solution.py:20
  163.2 25.0 %collective-permute-start.28 = (bf16[2,4,4,2,64,128]{5,4,3,2,1,0:T(8,128)(2,1)}, bf16[2,4,4,2,64,128]{5,4,3,2,1,0:T(8,128)(2,1)}, u32[]{:S(2)}, u32[]{:S(2)}) collective-permute-start(bf16[2,4,4,2,64,128]{5,4,3,2,1,0:T(8,128)(2,1)} %collective-permute-done.27.refs_5_), channel_id=1, source_target_pairs={{2,0},{4,2},{6,4},{0,6},{3,1},{5,3},{7,5},{1,7},{10,8},{12,10},{14... | collective-permute-start | bytes 3145736 | tf_op jit(solution)/shard_map/ppermute | solution.py:20
  170.7 8.7 %collective-permute-start.22 = (bf16[16,8,1024]{2,1,0:T(8,128)(2,1)}, bf16[16,8,1024]{2,1,0:T(8,128)(2,1)S(1)}, u32[]{:S(2)}, u32[]{:S(2)}) collective-permute-start(bf16[16,8,1024]{2,1,0:T(8,128)(2,1)} %slice.275), channel_id=1, source_target_pairs={{224,0},{0,32},{32,64},{64,96},{96,128},{128,160},{160,192},{192,2... | collective-permute-start | bytes 786440 | tf_op jit(solution)/shard_map/ppermute | solution.py:20
  183.1 5.1 %collective-permute-start.23 = (bf16[4,256,256]{2,1,0:T(8,128)(2,1)S(1)}, bf16[4,256,256]{2,1,0:T(8,128)(2,1)S(1)}, u32[]{:S(2)}, u32[]{:S(2)}) collective-permute-start(bf16[4,256,256]{2,1,0:T(8,128)(2,1)S(1)} %get-tuple-element.21.own), channel_id=1, source_target_pairs={{0,1},{1,0},{2,3},{3,2},{4,5},{5,4},{6,7},{7,6},{8,9},{9,8},{10,11... | collective-permute-start | bytes 1572872 | tf_op jit(solution)/shard_map/ppermute | solution.py:24
  200.3 3.7 %collective-permute-start.30 = (bf16[256,1024]{1,0:T(8,128)(2,1)S(1)}, bf16[256,1024]{1,0:T(8,128)(2,1)S(1)}, u32[]{:S(2)}, u32[]{:S(2)}) collective-permute-start(bf16[256,1024]{1,0:T(8,128)(2,1)S(1)} %get-tuple-element.25), channel_id=1, source_target_pairs={{0,1},{1,0},{2,3},{3,2},{4,5},{5,4},{6,7},{7,6},{8,9},{9,8},{10,11... | collective-permute-start | bytes 1572872 | tf_op jit(solution)/shard_map/ppermute | solution.py:24
  (11 other events, 64.7 us)
